TPU v7x, 32 devices: a whole 2x2x4 slice. The times are simulated.
32 devices in a mesh: batch: 16 (over z, x, core), seq: 2 (over y).
Axes of the slice: x: 2, y: 2, z: 4, core: 2. Of those that a mesh axis runs over, the one named last changes fastest.
Arguments:
- tokens: bfloat16 [16, 1024, 2560], P('batch', 'seq'), may hold values from -6 to 6
- attn_in: bfloat16 [16, 1024, 2560], P('batch', 'seq'), may hold values from -6 to 6
- lengths: int32 [16], P('batch'), may hold values from 256 to 1024
- norm_gain: float32 [2560], replicated, may hold values from 0.5 to 1.5
- attn_gain: float32 [2560], replicated, may hold values from 0.5 to 1.5
- w_x: bfloat16 [2560, 2560], P(('batch', 'seq')), may hold values from -0.125 to 0.125
- conv_w: float32 [4, 2560], replicated, may hold values from -3 to 3
- w_a: bfloat16 [10, 256, 256], replicated, may hold values from -0.375 to 0.375
- w_i: bfloat16 [10, 256, 256], replicated, may hold values from -0.375 to 0.375
- lru_decay: float32 [2560], replicated, may hold values from 4 to 20
- w_kv: bfloat16 [2560, 512], replicated, may hold values from -0.125 to 0.125
Outputs:
- lru_state: float32 [16, 2560], P('batch', 'seq')
- conv_state: bfloat16 [16, 3, 2560], P('batch', None, 'seq')
- kv_cache: bfloat16 [16, 2048, 512], P('batch', None, 'seq')
Inputs may be any that keep to these rules, and one draw needn't show every extreme that they name: `lengths`: positions from a prompt's length on are padding.
All inputs are finite; a program needn't handle non-finite values.
Results may differ from a plain program's by a relative error of at most 0.0051.
Values may be sent and summed in bfloat16 or wider, within the bound.
A program may use at most 128 MiB of HBM per device.

v0:
```python
import functools

import jax
import jax.numpy as jnp
from jax import lax
from jax.experimental import pallas as pl
from jax.experimental.pallas import tpu as pltpu
from jax.sharding import PartitionSpec as P

H = 10
HD = 256
W = 2048
LANES_OF_TIME = 8
TAPS = 4
HALO = 16
STEP_ROWS = 32


def passed_along(block, axis, distance):
    devices = range(lax.axis_size(axis))
    route = [(i - distance, i) for i in devices if i - distance in devices]
    return lax.ppermute(block, axis, route)


def rms_norm(values, gain_vec):
    widened = values.astype(jnp.float32)
    inverse = lax.rsqrt(jnp.mean(widened * widened, axis=-1, keepdims=True) + 1e-06)
    return (widened * inverse * gain_vec).astype(jnp.bfloat16)


def rotate_keys(key_rows, positions):
    quarter = key_rows.shape[-1] // 4
    spacing = jnp.exp(-jnp.log(10000.0) * jnp.arange(quarter, dtype=jnp.float32) / quarter)
    angles = positions.astype(jnp.float32)[:, None] * spacing[None, :]
    cosine_rows = jnp.cos(angles)
    sine_rows = jnp.sin(angles)
    first_part = key_rows[:, :quarter]
    second_part = key_rows[:, quarter : 2 * quarter]
    return jnp.concatenate(
        [
            first_part * cosine_rows - second_part * sine_rows,
            second_part * cosine_rows + first_part * sine_rows,
            key_rows[:, 2 * quarter :],
        ],
        axis=1,
    )


def ordered_rows(tokens_ref, halo_ref, gain_ref, normed_ref):
    local_len = tokens_ref.shape[0]
    steps = local_len // LANES_OF_TIME
    row = lax.broadcasted_iota(jnp.int32, (normed_ref.shape[0], local_len + HALO), 0)
    col = lax.broadcasted_iota(jnp.int32, (normed_ref.shape[0], local_len + HALO), 1)
    at = lax.rem(row, LANES_OF_TIME) * steps + lax.div(row, LANES_OF_TIME) - (TAPS - 1)
    pick = (jnp.where(at < 0, at + local_len + HALO, at) == col).astype(jnp.bfloat16)
    rows = jnp.concatenate(
        [rms_norm(tokens_ref[...], gain_ref[...]), rms_norm(halo_ref[...], gain_ref[...])], axis=0
    )
    normed_ref[...] = jnp.dot(pick, rows, preferred_element_type=jnp.float32).astype(jnp.bfloat16)


def one_head(
    normed_ref, w_block, conv_w, w_a, w_i, rate, length, start, out_ref, xp_ref, xc_ref, ga_ref, gi_ref
):
    rows_ext = normed_ref.shape[0]
    local_len = xc_ref.shape[0]
    steps = local_len // LANES_OF_TIME
    projected = jnp.dot(normed_ref[...], w_block, preferred_element_type=jnp.float32).astype(
        jnp.bfloat16
    )
    xp_ref[...] = projected.astype(jnp.float32)
    row = lax.broadcasted_iota(jnp.int32, (HALO, rows_ext), 1)
    wanted = length - (TAPS - 1) + lax.broadcasted_iota(jnp.int32, (HALO, rows_ext), 0) - 2
    step = lax.div(row, LANES_OF_TIME) - (TAPS - 1)
    at = start + lax.rem(row, LANES_OF_TIME) * steps + step
    real = (step >= 0) & (step < steps) & (wanted < length) & (wanted >= length - (TAPS - 1))
    picker = (real & (at == wanted)).astype(jnp.bfloat16)
    picked = jnp.dot(picker, projected, preferred_element_type=jnp.float32)
    conv_sum = conv_w[0:1] * xp_ref[0:local_len]
    for offset in range(1, TAPS):
        shift = offset * LANES_OF_TIME
        conv_sum = conv_sum + conv_w[offset : offset + 1] * xp_ref[shift : shift + local_len]
    x_conv = conv_sum.astype(jnp.bfloat16)
    xc_ref[...] = x_conv.astype(jnp.float32)
    ga_ref[...] = jnp.dot(x_conv, w_a, preferred_element_type=jnp.float32)
    gi_ref[...] = jnp.dot(x_conv, w_i, preferred_element_type=jnp.float32)
    inner = lax.broadcasted_iota(jnp.int32, (STEP_ROWS, HD), 0)
    first_at = start + lax.rem(inner, LANES_OF_TIME) * steps + lax.div(inner, LANES_OF_TIME)

    def block(i, carry):
        state, rate_sum = carry
        rows = pl.ds(pl.multiple_of(i * STEP_ROWS, STEP_ROWS), STEP_ROWS)
        valid = first_at + i * (STEP_ROWS // LANES_OF_TIME) < length
        log_rate = rate * jax.nn.sigmoid(ga_ref[rows])
        fall = -2.0 * log_rate
        lost = 1.0 - fall * (1.0 / 6.0)
        for order in (5.0, 4.0, 3.0, 2.0):
            lost = 1.0 - fall * (1.0 / order) * lost
        lost = fall * lost
        root = lost * lax.rsqrt(jnp.maximum(lost, 1e-37))
        push = jnp.where(valid, root * jax.nn.sigmoid(gi_ref[rows]) * xc_ref[rows], 0.0)
        held = jnp.where(valid, log_rate, 0.0)
        keep = jnp.exp(held)
        for k in range(STEP_ROWS // LANES_OF_TIME):
            tile = slice(k * LANES_OF_TIME, (k + 1) * LANES_OF_TIME)
            state = keep[tile] * state + push[tile]
            rate_sum = rate_sum + held[tile]
        return state, rate_sum

    zeros = jnp.zeros((LANES_OF_TIME, HD), jnp.float32)
    state, rate_sum = lax.fori_loop(0, local_len // STEP_ROWS, block, (zeros, zeros))
    keep_all = jnp.exp(rate_sum)
    total = state[0:1]
    for s in range(1, LANES_OF_TIME):
        total = keep_all[s : s + 1] * total + state[s : s + 1]
    keep_total = jnp.exp(jnp.sum(rate_sum, axis=0, keepdims=True))
    place = lax.broadcasted_iota(jnp.int32, (LANES_OF_TIME, HD), 0)
    out_ref[...] = jnp.where(
        place == 0, keep_total, jnp.where(place == 1, total, picked[0:LANES_OF_TIME])
    )


def recurrent_kernel(
    length_ref,
    tokens_ref,
    halo_ref,
    gain_ref,
    w_ref,
    conv_ref,
    wa_ref,
    wi_ref,
    rate_ref,
    out_ref,
    normed_ref,
    *work
):
    @pl.when(pl.program_id(0) == 0)
    def _():
        ordered_rows(tokens_ref, halo_ref, gain_ref, normed_ref)

    start = lax.axis_index("seq") * tokens_ref.shape[0]
    one_head(
        normed_ref,
        w_ref[...],
        conv_ref[...],
        wa_ref[0],
        wi_ref[0],
        rate_ref[...],
        length_ref[0],
        start,
        out_ref,
        *work
    )


def recurrent(first, tokens, halo, lengths, norm_gain, w_part, conv_w, w_a, w_i, rate):
    local_len, width = tokens.shape
    part_width = w_part.shape[1]
    rows_ext = -(-(local_len + (TAPS - 1) * LANES_OF_TIME) // HALO) * HALO
    whole = lambda *shape: pl.BlockSpec(shape, lambda h: (0,) * len(shape))
    return pl.pallas_call(
        recurrent_kernel,
        grid=(part_width // HD,),
        in_specs=[
            pl.BlockSpec(memory_space=pltpu.SMEM),
            whole(local_len, width),
            whole(HALO, width),
            whole(1, width),
            pl.BlockSpec((width, HD), lambda h: (0, h)),
            pl.BlockSpec((TAPS, HD), lambda h: (0, h + first)),
            pl.BlockSpec((1, HD, HD), lambda h: (h + first, 0, 0)),
            pl.BlockSpec((1, HD, HD), lambda h: (h + first, 0, 0)),
            pl.BlockSpec((1, HD), lambda h: (0, h + first)),
        ],
        out_specs=pl.BlockSpec((LANES_OF_TIME, HD), lambda h: (0, h)),
        out_shape=jax.ShapeDtypeStruct((LANES_OF_TIME, part_width), jnp.float32),
        scratch_shapes=[
            pltpu.VMEM((rows_ext, width), jnp.bfloat16),
            pltpu.VMEM((rows_ext, HD), jnp.float32),
            pltpu.VMEM((local_len, HD), jnp.float32),
            pltpu.VMEM((local_len, HD), jnp.float32),
            pltpu.VMEM((local_len, HD), jnp.float32),
        ],
        compiler_params=pltpu.CompilerParams(vmem_limit_bytes=60 * 1024 * 1024),
        cost_estimate=pl.CostEstimate(
            flops=2 * local_len * part_width * (width + 2 * HD),
            bytes_accessed=2 * width * (local_len + part_width),
            transcendentals=6 * local_len * part_width,
        ),
    )(lengths, tokens, halo, norm_gain[None], w_part, conv_w, w_a, w_i, rate[None])


def on_device(
    tokens, attn_in, lengths, norm_gain, attn_gain, w_x, conv_w, w_a, w_i, lru_decay, w_kv
):
    local_len = tokens.shape[1]
    feature_dim = tokens.shape[2]
    seq_parts = lax.axis_size("seq")
    seq_place = lax.axis_index("seq")
    length = lengths[0]
    halo = passed_along(tokens[0, local_len - HALO :], "seq", 1)
    heads = feature_dim // HD
    early = (4 * heads) // 5
    positions = seq_place * local_len + jnp.arange(local_len, dtype=jnp.int32)
    attn_normed = rms_norm(attn_in[0], attn_gain)
    kv_full = jnp.dot(attn_normed, w_kv, preferred_element_type=jnp.float32)
    kv_rows = jnp.concatenate(
        [rotate_keys(kv_full[:, :HD], positions), kv_full[:, HD:]], axis=1
    ).astype(jnp.bfloat16)
    in_window = ((positions >= length - W) & (positions < length))[:, None]
    masked = jnp.where(in_window, kv_rows, jnp.zeros_like(kv_rows))
    by_column = lax.all_to_all(masked, "seq", split_axis=1, concat_axis=0, tiled=True)
    laps = -(-seq_parts * local_len // W)
    by_column = jnp.pad(by_column, ((0, laps * W - seq_parts * local_len), (0, 0)))
    kv_cache = by_column[:W]
    for lap in range(1, laps):
        kv_cache = kv_cache + by_column[lap * W : (lap + 1) * W]
    w_early = lax.all_gather(w_x[:, : early * HD], ("batch", "seq"), axis=0, tiled=True)
    w_early, w_local, kv_cache, halo = lax.optimization_barrier((w_early, w_x, kv_cache, halo))
    w_late = lax.all_gather(w_local[:, early * HD :], ("batch", "seq"), axis=0, tiled=True)
    w_parts = ((0, w_early), (early, w_late))
    rate = -8.0 * jax.nn.softplus(-lru_decay)
    summary = jnp.concatenate(
        [
            recurrent(first, tokens[0], halo, lengths, norm_gain, w_part, conv_w, w_a, w_i, rate)
            for first, w_part in w_parts
        ],
        axis=1,
    )
    owned_width = feature_dim // seq_parts
    gathered = lax.all_gather(summary, "seq", axis=0, tiled=True)
    owned = lax.dynamic_slice_in_dim(gathered, seq_place * owned_width, owned_width, 1)
    state = owned[1:2]
    picked = owned[2:5]
    for part in range(1, seq_parts):
        at = part * LANES_OF_TIME
        state = owned[at : at + 1] * state + owned[at + 1 : at + 2]
        picked = picked + owned[at + 2 : at + 5]
    conv_state = picked.astype(jnp.bfloat16)
    return (state, conv_state[None], kv_cache[None])


def solution(mesh):
    in_specs = (
        P("batch", "seq", None),
        P("batch", "seq", None),
        P("batch"),
        P(),
        P(),
        P(("batch", "seq"), None),
        P(),
        P(),
        P(),
        P(),
        P(),
    )
    out_specs = (P("batch", "seq"), P("batch", None, "seq"), P("batch", None, "seq"))
    return jax.shard_map(
        on_device, mesh=mesh, in_specs=in_specs, out_specs=out_specs, check_vma=False
    )
```

profile of v0, /device:TPU:0, one launch (start us, length us, event | category | flops | bytes accessed | tf_op | source)
XLA Modules:
  0.0 185.7 jit_solution(8690938932169258410)
XLA Ops:
  7.2 0.0 all-gather.3.cloned.1.call-start
  7.2 1.9 %slice.40 = bf16[80,2048]{1,0:T(8,128)(2,1)} slice(bf16[80,2560]{1,0:T(8,128)(2,1)} %param.16), slice={[0:80], [0:2048]} | slice | bytes 655360 | tf_op jit(solution)/shard_map/slice | solution.py:218
  9.1 2.5 %fusion = f32[512]{0:T(512)S(1)} fusion(bf16[1,512,2560]{2,1,0:T(8,128)(2,1)} %param.12), kind=kLoop, calls=%fused_computation.2 | loop fusion | flops 3931648 | bytes 2623488 | tf_op jit(solution)/shard_map/reduce_sum | solution.py:27
  11.7 1.7 fusion.3
  13.3 1.0 copy-done.2
  15.0 1.5 fusion.13
  16.7 0.8 broadcast_select_fusion
  17.5 4.3 %all-to-all-start = ((bf16[512,2,256]{0,2,1:T(8,128)(2,1)}), bf16[512,2,256]{0,2,1:T(8,128)(2,1)S(1)}, u32[]{:S(2)}, u32[]{:S(2)}) async-start(bf16[512,2,256]{0,2,1:T(8,128)(2,1)} %broadcast_select_fusion), calls=%async_computation | async-start | bytes 1048576 | tf_op jit(solution)/shard_map/all_to_all | solution.py:212
  21.8 0.9 slice_bitcast_fusion
  22.7 4.2 %collective-permute-start = (bf16[16,2560]{1,0:T(8,128)(2,1)S(1)}, bf16[16,2560]{1,0:T(8,128)(2,1)S(1)}, u32[]{:S(2)}, u32[]{:S(2)}) collective-permute-start(bf16[16,2560]{1,0:T(8,128)(2,1)S(1)} %slice_bitcast_fusion), channel_id=1, source_target_pairs={{0,1},{2,3},{4,5},{6,7},{8,9},{10,11},{12,13},{14,15},{16,17},{18,... | collective-permute-start | bytes 245768 | tf_op jit(solution)/shard_map/ppermute | solution.py:22
  26.8 6.0 %all-to-all-done = bf16[512,2,256]{0,2,1:T(8,128)(2,1)S(1)} async-done(((bf16[512,2,256]{0,2,1:T(8,128)(2,1)}), bf16[512,2,256]{0,2,1:T(8,128)(2,1)S(1)}, u32[]{:S(2)}, u32[]{:S(2)}) %all-to-all-start) | async-done | bytes 524320 | tf_op jit(solution)/shard_map/all_to_all | solution.py:212
  32.8 1.0 copy.14
  33.8 2.1 %pad.4 = bf16[2048,256]{1,0:T(8,128)(2,1)} pad(bf16[1024,256]{1,0:T(8,128)(2,1)} %bitcast.24, bf16[]{:T(256)} %constant.11.clone.1), padding=0_1024x0_0 | pad | bytes 1572866 | tf_op jit(solution)/shard_map/jit(_pad)/pad | solution.py:214
  35.9 65.6 %all-gather.3.cloned.1.call-done.w_ref = bf16[2560,2048]{1,0:T(8,128)(2,1)} async-done(((bf16[80,2048]{1,0:T(8,128)(2,1)}), bf16[2560,2048]{1,0:T(8,128)(2,1)}) %all-gather.3.cloned.1.call-update) | async-done | bytes 10485776 | tf_op jit(solution)/shard_map/all_gather | solution.py:218
  101.5 1.5 slice.45
  103.1 0.6 broadcast_in_dim.33.rate_ref
  103.7 0.6 broadcast_in_dim.32.gain_ref
  104.3 25.3 %shard_map.130 = f32[8,2048]{1,0:T(8,128)} custom-call(s32[1]{0:T(128)} %copy.15.length_ref, bf16[512,2560]{1,0:T(8,128)(2,1)} %bitcast.20, bf16[16,2560]{1,0:T(8,128)(2,1)} %copy-done.3, f32[1,2560]{1,0:T(1,128)} %broadcast_in_dim.32.gain_ref, bf16[2560,2048]{1,0:T(8,128)(2,1)} %all-gather.3.cloned.1.call-done.w_ref, f32[4,2560]{1,0:T(4,128)} %conv_ref.3, ...), custom_call_target="tpu_custom_call" | custom-call | flops 6442450944 | bytes 13107200 | tf_op jit(solution)/shard_map/pallas_call | solution.py:161
  129.6 31.2 %all-gather.5.cloned.1.call-done.w_ref = bf16[2560,512]{1,0:T(8,128)(2,1)} async-done(((bf16[80,512]{1,0:T(8,128)(2,1)}), bf16[2560,512]{1,0:T(8,128)(2,1)}) %all-gather.5.cloned.1.call-update) | async-done | bytes 2621456 | tf_op jit(solution)/shard_map/all_gather | solution.py:220
  160.8 10.8 %shard_map.131 = f32[8,512]{1,0:T(8,128)} custom-call(s32[1]{0:T(128)} %copy.15.length_ref, bf16[512,2560]{1,0:T(8,128)(2,1)} %bitcast.21, bf16[16,2560]{1,0:T(8,128)(2,1)} %copy-done.3, f32[1,2560]{1,0:T(1,128)} %broadcast_in_dim.32.gain_ref, bf16[2560,512]{1,0:T(8,128)(2,1)} %all-gather.5.cloned.1.call-done.w_ref, f32[4,2560]{1,0:T(4,128)} %conv_ref.3, ...), custom_call_target="tpu_custom_call" | custom-call | flops 1610612736 | bytes 5242880 | tf_op jit(solution)/shard_map/pallas_call | solution.py:161
  171.6 0.7 pad_maximum_fusion.1
  172.3 5.2 %all_gather.11 = f32[16,2560]{1,0:T(8,128)S(1)} all-gather(f32[8,2560]{1,0:T(8,128)S(1)} %pad_maximum_fusion.1), channel_id=1, replica_groups=mesh['batch'=16,'seq'=2] {'seq'}, dimensions={0}, use_global_device_ids=true | all-gather | bytes 245760 | tf_op jit(solution)/shard_map/all_gather | solution.py:231
  177.5 0.7 fusion.18
  178.2 0.7 dynamic-slice_add_fusion.1
  (26 shorter events, 0.2 us)
Async XLA Ops:
  7.2 4.5 %copy-start = (bf16[2560,512]{1,0:T(8,128)(2,1)S(1)}, bf16[2560,512]{1,0:T(8,128)(2,1)}, u32[]{:S(2)}) copy-start(bf16[2560,512]{1,0:T(8,128)(2,1)} %param.21) | copy-start | bytes 7864324
  7.2 4.5 %copy-start.7 = (f32[2560]{0:T(1024)S(1)}, f32[2560]{0:T(1024)}, u32[]{:S(2)}) copy-start(f32[2560]{0:T(1024)} %param.15) | copy-start | bytes 30724
  7.2 94.3 %all-gather.3.cloned.1.call-start = ((), (), s32[]{:S(2)}) async-start(), calls=%async_computation.1 | async-start | bytes 10813440 | tf_op jit(solution)/shard_map/all_gather | solution.py:218
  9.1 2.5 %copy-start.1 = (bf16[1,512,2560]{2,1,0:T(8,128)(2,1)S(1)}, bf16[1,512,2560]{2,1,0:T(8,128)(2,1)}, u32[]{:S(2)}) copy-start(bf16[1,512,2560]{2,1,0:T(8,128)(2,1)} %param.12) | copy-start | bytes 7864324
  13.3 1.0 copy-start.2
  16.6 86.4 %copy-start.5 = (f32[2560]{0:T(1024)S(1)}, f32[2560]{0:T(1024)}, u32[]{:S(2)}) copy-start(f32[2560]{0:T(1024)} %param.20) | copy-start | bytes 30724
  16.6 87.1 %copy-start.6 = (f32[2560]{0:T(1024)S(1)}, f32[2560]{0:T(1024)}, u32[]{:S(2)}) copy-start(f32[2560]{0:T(1024)} %param.14) | copy-start | bytes 30724
  17.5 15.3 %all-to-all-start = ((bf16[512,2,256]{0,2,1:T(8,128)(2,1)}), bf16[512,2,256]{0,2,1:T(8,128)(2,1)S(1)}, u32[]{:S(2)}, u32[]{:S(2)}) async-start(bf16[512,2,256]{0,2,1:T(8,128)(2,1)} %broadcast_select_fusion), calls=%async_computation | async-start | bytes 1048576 | tf_op jit(solution)/shard_map/all_to_all | solution.py:212
  21.7 139.0 %all-gather.5.cloned.1.call-start = ((), (), s32[]{:S(2)}) async-start(), calls=%async_computation.2 | async-start | bytes 2703360 | tf_op jit(solution)/shard_map/all_gather | solution.py:220
  22.7 13.3 %collective-permute-start = (bf16[16,2560]{1,0:T(8,128)(2,1)S(1)}, bf16[16,2560]{1,0:T(8,128)(2,1)S(1)}, u32[]{:S(2)}, u32[]{:S(2)}) collective-permute-start(bf16[16,2560]{1,0:T(8,128)(2,1)S(1)} %slice_bitcast_fusion), channel_id=1, source_target_pairs={{0,1},{2,3},{4,5},{6,7},{8,9},{10,11},{12,13},{14,15},{16,17},{18,... | collective-permute-start | bytes 245768 | tf_op jit(solution)/shard_map/ppermute | solution.py:22
  35.9 68.4 %copy-start.3 = (bf16[16,2560]{1,0:T(8,128)(2,1)}, bf16[16,2560]{1,0:T(8,128)(2,1)S(1)}, u32[]{:S(2)}) copy-start(bf16[16,2560]{1,0:T(8,128)(2,1)S(1)} %collective-permute-done.halo_ref) | copy-start | bytes 245764
  129.6 41.9 %copy-start.4 = (f32[8,2048]{1,0:T(8,128)S(1)}, f32[8,2048]{1,0:T(8,128)}, u32[]{:S(2)}) copy-start(f32[8,2048]{1,0:T(8,128)} %shard_map.130) | copy-start | bytes 196612
Sparse Core Ops, SparseCore 0:
  10.9 90.5 all-gather.2
  104.4 56.3 all-gather.4
where the time goes:
time: 186 us
  waiting for transfers between devices  103 us (55%)
  Pallas kernels  36.1 us (19%)
  between operations  14.8 us (8%)
  local copies, waits for them, and re-layouts  9.65 us (5%)
  starting transfers between devices  8.48 us (5%)
  other arithmetic  7.04 us (4%)
  blocking collectives  5.22 us (3%)
    all_gather x1, waiting for transfers between devices, on_device(): lax.all_gather(w_x[:, :early * HD], ('batch', 'seq'), axis=0, tiled=True)  65.6 us
    pallas_call x2, Pallas kernels, recurrent(): pl.pallas_call(recurrent_kernel, grid=(part_width // HD,), in_specs=[pl.B...  36.1 us
    all_gather x1, waiting for transfers between devices, on_device(): lax.all_gather(w_local[:, early * HD:], ('batch', 'seq'), axis=0, tiled=T...  31.2 us
    all_to_all x1, waiting for transfers between devices, on_device(): lax.all_to_all(masked, 'seq', split_axis=1, concat_axis=0, tiled=True)  5.99 us
    all_gather x1, blocking collectives, on_device(): gathered = lax.all_gather(summary, 'seq', axis=0, tiled=True)  5.22 us
    all_to_all x1, starting transfers between devices, on_device(): lax.all_to_all(masked, 'seq', split_axis=1, concat_axis=0, tiled=True)  4.26 us
    ppermute x1, starting transfers between devices, passed_along(): return lax.ppermute(block, axis, route)  4.18 us
  transfers between devices with their start and end apart: 4, of which 3 were waited for; matrix products, arithmetic and copies ran while one was open for 6% of the time, Pallas kernels for 14%

commit v1 on v0

--- a/solution.py
+++ b/solution.py
@@ -240,6 +240,647 @@
     return (state, conv_state[None], kv_cache[None])
 
 
+MESH_ID = pl.DeviceIdType.MESH
+PLANE_ROWS = 16
+CROSS_ROWS = 16
+NEAR, PLANE = 0, 1
+
+
+def physical_grid(mesh):
+    grid = mesh.devices
+    try:
+        spots = [
+            [(*device.coords, device.core_on_chip) for device in line] for line in grid.tolist()
+        ]
+    except AttributeError:
+        return None
+    sizes = [len({spot[k] for line in spots for spot in line}) for k in range(4)]
+    low = [min(spot[k] for line in spots for spot in line) for k in range(4)]
+    x_size, y_size, z_size, cores = sizes
+    if (x_size, y_size, z_size, cores) != (2, 2, 4, 2) or grid.shape != (z_size * x_size * cores, y_size):
+        return None
+    for b, line in enumerate(spots):
+        for y, spot in enumerate(line):
+            want = ((b // cores) % x_size, y, b // (cores * x_size), b % cores)
+            if tuple(v - l for v, l in zip(spot, low)) != want:
+                return None
+    return z_size, x_size, cores, y_size
+
+
+class Exchange:
+    def __init__(self, sizes, heads, w_buf, send_sem, recv_sem, core_send, core_recv):
+        self.sizes, self.heads = sizes, heads
+        self.w_buf, self.send_sem, self.recv_sem = w_buf, send_sem, recv_sem
+        self.core_send, self.core_recv = core_send, core_recv
+        z_size, x_size, cores, _ = sizes
+        at = lax.axis_index("batch")
+        self.core = lax.rem(at, cores)
+        self.x = lax.rem(lax.div(at, cores), x_size)
+        self.z = lax.div(at, cores * x_size)
+        self.y = lax.axis_index("seq")
+        self.shard_rows = w_buf.shape[5]
+        self.near_rows = self.shard_rows - PLANE_ROWS
+        self.is_end = (self.z == 0) | (self.z == z_size - 1)
+
+    def device(self, z=None, x=None, core=None, y=None):
+        z = self.z if z is None else z
+        x = self.x if x is None else x
+        core = self.core if core is None else core
+        y = self.y if y is None else y
+        _, x_size, cores, _ = self.sizes
+        return ((z * x_size + x) * cores + core, y)
+
+    def peers(self):
+        z_size = self.sizes[0]
+        along = [self.device(z=lax.rem(self.z + d, z_size)) for d in range(1, z_size)]
+        return along + [
+            self.device(x=1 - self.x),
+            self.device(y=1 - self.y),
+            self.device(x=1 - self.x, y=1 - self.y),
+            self.device(core=1 - self.core),
+        ]
+
+    def blocks(self, head, z, x, y, first, rows, core=None):
+        core = self.core if core is None else core
+        return self.w_buf.at[head, z, x, core, y, pl.ds(first, rows)]
+
+    def copy(self, head, stage, group, part, to):
+        return pltpu.make_async_remote_copy(
+            src_ref=part,
+            dst_ref=part,
+            send_sem=self.send_sem.at[head, stage, group],
+            recv_sem=self.recv_sem.at[head, stage, group],
+            device_id=to,
+            device_id_type=MESH_ID,
+        )
+
+    def hand_over(self, head, part):
+        pltpu.make_async_remote_copy(
+            src_ref=part,
+            dst_ref=part,
+            send_sem=self.core_send.at[head],
+            recv_sem=self.core_recv.at[head],
+            device_id=self.device(core=1 - self.core),
+            device_id_type=MESH_ID,
+        ).start()
+
+    def some(self, head, count, rows):
+        every = slice(None)
+        if count == 3:
+            return self.w_buf.at[head, pl.ds(0, 3), 0, 0, 0, pl.ds(0, rows)]
+        if count == 4:
+            return self.w_buf.at[head, every, 0, 0, 0, pl.ds(0, rows)]
+        if count == 8:
+            return self.w_buf.at[head, every, every, 0, 0, pl.ds(0, rows)]
+        return self.w_buf.at[head, pl.ds(0, 3), every, 0, every, pl.ds(0, rows)]
+
+    def arrived(self, head, stage, group, count, rows):
+        self.copy(head, stage, group, self.some(head, count, rows), self.device(core=1 - self.core)).wait_recv()
+
+    def left(self, head, stage, group, count, rows):
+        self.copy(head, stage, group, self.some(head, count, rows), self.device(core=1 - self.core)).wait_send()
+
+    def routes(self, act):
+        near = (PLANE_ROWS, self.near_rows)
+
+        @pl.when(self.core == 0)
+        def _():
+            act("yx", PLANE_ROWS, CROSS_ROWS)
+            act("xy", PLANE_ROWS + CROSS_ROWS, self.near_rows - CROSS_ROWS)
+
+        @pl.when(self.core != 0)
+        def _():
+            act("yx", *near)
+
+    def first(self, head):
+        z_size = self.sizes[0]
+        near = self.blocks(head, self.z, self.x, self.y, PLANE_ROWS, self.near_rows)
+        for d in range(1, z_size):
+            self.copy(head, 0, NEAR, near, self.device(z=lax.rem(self.z + d, z_size))).start()
+        plane = self.blocks(head, self.z, self.x, self.y, 0, PLANE_ROWS)
+        self.copy(head, 0, PLANE, plane, self.device(x=1 - self.x)).start()
+        self.copy(head, 0, PLANE, plane, self.device(y=1 - self.y)).start()
+        self.copy(head, 0, PLANE, plane, self.device(x=1 - self.x, y=1 - self.y)).start()
+
+    def second(self, head):
+        every = slice(None)
+        last = self.sizes[0] - 1
+        self.arrived(head, 0, NEAR, 3, self.near_rows)
+
+        def near(order, first, rows):
+            part = self.blocks(head, every, self.x, self.y, first, rows)
+            to = self.device(x=1 - self.x) if order == "xy" else self.device(y=1 - self.y)
+            self.copy(head, 1, NEAR, part, to).start()
+
+        self.routes(near)
+        self.arrived(head, 0, PLANE, 3, PLANE_ROWS)
+        plane = self.blocks(head, self.z, every, every, 0, PLANE_ROWS)
+        up = jnp.where(self.z == last, 1, self.z + 1)
+        down = jnp.where(self.z == 0, last - 1, self.z - 1)
+        self.copy(head, 1, PLANE, plane, self.device(z=up)).start()
+        self.copy(head, 1, PLANE, plane, self.device(z=down)).start()
+        self.hand_over(head, plane)
+
+    def third(self, head):
+        every = slice(None)
+        last = self.sizes[0] - 1
+        self.arrived(head, 1, NEAR, 4, self.near_rows)
+
+        def near(order, first, rows):
+            if order == "xy":
+                part = self.blocks(head, every, every, self.y, first, rows)
+                to = self.device(y=1 - self.y)
+            else:
+                part = self.blocks(head, every, self.x, every, first, rows)
+                to = self.device(x=1 - self.x)
+            self.copy(head, 2, NEAR, part, to).start()
+            self.hand_over(head, part)
+
+        self.routes(near)
+
+        @pl.when(self.is_end)
+        def _():
+            self.arrived(head, 1, PLANE, 4, PLANE_ROWS)
+
+        @pl.when(jnp.logical_not(self.is_end))
+        def _():
+            self.arrived(head, 1, PLANE, 12, PLANE_ROWS)
+            half = (last + 1) // 2
+            start = jnp.where(self.z >= half, 0, half)
+            part = self.blocks(head, pl.ds(start, half), every, every, 0, PLANE_ROWS)
+            self.copy(head, 2, PLANE, part, self.device(z=jnp.where(self.z >= half, last, 0))).start()
+
+    def fourth(self, head):
+        every = slice(None)
+        z_size = self.sizes[0]
+        self.arrived(head, 2, NEAR, 8, self.near_rows)
+
+        def near(order, first, rows):
+            if order == "xy":
+                part = self.blocks(head, every, every, 1 - self.y, first, rows)
+            else:
+                part = self.blocks(head, every, 1 - self.x, every, first, rows)
+            self.hand_over(head, part)
+
+        self.routes(near)
+
+        @pl.when(self.is_end)
+        def _():
+            self.arrived(head, 2, PLANE, 8, PLANE_ROWS)
+
+        for d in range(1, z_size):
+            self.hand_over(head, self.blocks(head, lax.rem(self.z + d, z_size), every, every, 0, PLANE_ROWS))
+
+    def handed(self, head, core):
+        every = slice(None)
+        part = self.w_buf.at[head, every, every, core]
+        return pltpu.make_async_remote_copy(
+            src_ref=part,
+            dst_ref=part,
+            send_sem=self.core_send.at[head],
+            recv_sem=self.core_recv.at[head],
+            device_id=self.device(core=1 - self.core),
+            device_id_type=MESH_ID,
+        )
+
+    def ready(self, head):
+        self.handed(head, 1 - self.core).wait_recv()
+
+    def settled(self, head):
+        self.left(head, 0, NEAR, 3, self.near_rows)
+        self.left(head, 0, PLANE, 3, PLANE_ROWS)
+        self.left(head, 1, NEAR, 4, self.near_rows)
+        self.left(head, 1, PLANE, 8, PLANE_ROWS)
+        self.left(head, 2, NEAR, 8, self.near_rows)
+
+        @pl.when(jnp.logical_not(self.is_end))
+        def _():
+            self.left(head, 2, PLANE, 8, PLANE_ROWS)
+
+        self.handed(head, self.core).wait_send()
+
+
+def prefill_kernel(
+    sizes,
+    length_ref,
+    tokens_hbm,
+    attn_hbm,
+    norm_gain_ref,
+    attn_gain_ref,
+    w_hbm,
+    conv_ref,
+    wa_hbm,
+    wi_hbm,
+    decay_ref,
+    wkv_hbm,
+    state_ref,
+    cache_ref,
+    w_buf,
+    tokens_v,
+    attn_v,
+    wkv_v,
+    wa_v,
+    wi_v,
+    halo_v,
+    rows_v,
+    normed_v,
+    kv_v,
+    zeros_v,
+    xp_v,
+    xc_v,
+    ga_v,
+    gi_v,
+    summary_v,
+    theirs_v,
+    turn_v,
+    send_sem,
+    recv_sem,
+    core_send,
+    core_recv,
+    load_sem,
+    side_send,
+    side_recv,
+):
+    heads = w_buf.shape[0]
+    local_len = tokens_v.shape[0]
+    seq_parts = sizes[3]
+    ex = Exchange(sizes, heads, w_buf, send_sem, recv_sem, core_send, core_recv)
+    y = ex.y
+    start = y * local_len
+    beside = ex.device(y=1 - y)
+
+    shard = [
+        pltpu.make_async_copy(
+            w_hbm.at[:, pl.ds(h * HD, HD)], w_buf.at[h, ex.z, ex.x, ex.core, y], load_sem.at[h]
+        )
+        for h in range(heads)
+    ]
+    loads = [
+        pltpu.make_async_copy(source, target, load_sem.at[heads + i])
+        for i, (source, target) in enumerate(
+            (
+                (tokens_hbm, tokens_v),
+                (attn_hbm, attn_v),
+                (wkv_hbm, wkv_v),
+                (wa_hbm, wa_v),
+                (wi_hbm, wi_v),
+            )
+        )
+    ]
+    for copy in shard + [loads[1], loads[2], loads[0], loads[3], loads[4]]:
+        copy.start()
+
+    barrier = pltpu.get_barrier_semaphore()
+    peers = ex.peers()
+    for peer in peers:
+        pl.semaphore_signal(barrier, inc=1, device_id=peer, device_id_type=MESH_ID)
+
+    zeros_v[...] = jnp.zeros_like(zeros_v)
+    quarter = HD // 4
+    lane = lax.broadcasted_iota(jnp.int32, (1, 2 * quarter), 1)
+    spacing = jnp.exp(
+        (-jnp.log(10000.0) / quarter) * lax.rem(lane, quarter).astype(jnp.float32)
+    )
+    half_len = local_len // 2
+    fine = lax.broadcasted_iota(jnp.int32, (half_len, 2 * quarter), 0).astype(jnp.float32) * spacing
+    turn_v[0] = jnp.cos(fine)
+    turn_v[1] = jnp.sin(fine)
+
+    for copy in shard:
+        copy.wait()
+    pl.semaphore_wait(barrier, len(peers))
+    for h in range(4):
+        ex.first(h)
+
+    length = length_ref[0]
+
+    def kv_half(k):
+        rows = slice(k * half_len, (k + 1) * half_len)
+        normed = rms_norm(attn_v[rows], attn_gain_ref[...])
+        full = jnp.dot(normed, wkv_v[...], preferred_element_type=jnp.float32)
+        place = start + k * half_len
+        coarse = place.astype(jnp.float32) * spacing
+        cos_c, sin_c = jnp.cos(coarse), jnp.sin(coarse)
+        cosine = cos_c * turn_v[0] - sin_c * turn_v[1]
+        sine = sin_c * turn_v[0] + cos_c * turn_v[1]
+        sine = jnp.where(lane < quarter, -sine, sine)
+        at = place + lax.broadcasted_iota(jnp.int32, (half_len, 1), 0)
+        window = (at >= length - W) & (at < length)
+        turned = full[:, : 2 * quarter]
+        other = pltpu.roll(turned, quarter, axis=1)
+        turned = turned * cosine + other * sine
+
+        def put(half, columns, values):
+            kv_v[half, rows, columns] = jnp.where(window, values, 0.0).astype(jnp.bfloat16)
+
+        put(0, slice(0, 2 * quarter), turned)
+        put(0, slice(2 * quarter, HD), full[:, 2 * quarter : HD])
+        put(1, slice(0, HD), full[:, HD:])
+
+    halo_copy = pltpu.make_async_remote_copy(
+        src_ref=tokens_v.at[pl.ds(local_len - HALO, HALO)],
+        dst_ref=halo_v,
+        send_sem=side_send.at[0],
+        recv_sem=side_recv.at[0],
+        device_id=beside,
+        device_id_type=MESH_ID,
+    )
+    loads[1].wait()
+    loads[2].wait()
+    kv_half(0)
+    ex.second(0)
+    loads[0].wait()
+
+    @pl.when(y == 0)
+    def _():
+        halo_copy.start()
+        halo_v[...] = jnp.zeros_like(halo_v)
+
+    kv_half(1)
+    ex.third(0)
+    ex.second(1)
+    kv_copy = pltpu.make_async_remote_copy(
+        src_ref=kv_v.at[1 - y],
+        dst_ref=cache_ref.at[pl.ds(start, local_len)],
+        send_sem=side_send.at[1],
+        recv_sem=side_recv.at[1],
+        device_id=beside,
+        device_id_type=MESH_ID,
+    )
+    kv_copy.start()
+    kept = pltpu.make_async_copy(kv_v.at[y], cache_ref.at[pl.ds(start, local_len)], load_sem.at[heads + 5])
+    kept.start()
+    rest = seq_parts * local_len
+    blank = pltpu.make_async_copy(
+        zeros_v, cache_ref.at[pl.ds(rest, cache_ref.shape[0] - rest)], load_sem.at[heads + 6]
+    )
+    blank.start()
+
+    norm_step = 64
+
+    def norm_rows(i, carry):
+        rows = pl.ds(pl.multiple_of(i * norm_step, norm_step), norm_step)
+        rows_v[rows] = rms_norm(tokens_v[rows], norm_gain_ref[...])
+        return carry
+
+    lax.fori_loop(0, local_len // norm_step, norm_rows, 0)
+    ex.second(2)
+    ex.third(1)
+
+    @pl.when(y != 0)
+    def _():
+        halo_copy.wait_recv()
+
+    steps = local_len // LANES_OF_TIME
+    rows_ext = normed_v.shape[0]
+    row = lax.broadcasted_iota(jnp.int32, (rows_ext, local_len), 0)
+    col = lax.broadcasted_iota(jnp.int32, (rows_ext, local_len), 1)
+    at = lax.rem(row, LANES_OF_TIME) * steps + lax.div(row, LANES_OF_TIME) - (TAPS - 1)
+    pick = (at == col).astype(jnp.bfloat16)
+
+    def reorder(i, carry):
+        columns = pl.ds(pl.multiple_of(i * HD, HD), HD)
+        normed_v[:, columns] = jnp.dot(
+            pick, rows_v[:, columns], preferred_element_type=jnp.float32
+        ).astype(jnp.bfloat16)
+        return carry
+
+    lax.fori_loop(0, heads, reorder, 0)
+    edge = 2 * HALO
+    row = lax.broadcasted_iota(jnp.int32, (edge, HALO), 0)
+    col = lax.broadcasted_iota(jnp.int32, (edge, HALO), 1)
+    at = lax.div(row, LANES_OF_TIME) - (TAPS - 1)
+    early = ((lax.rem(row, LANES_OF_TIME) == 0) & (at < 0) & (at + HALO == col)).astype(jnp.bfloat16)
+    halo_rows = rms_norm(halo_v[...], norm_gain_ref[...])
+    before = jnp.dot(early, halo_rows, preferred_element_type=jnp.float32)
+    normed_v[0:edge] = (normed_v[0:edge].astype(jnp.float32) + before).astype(jnp.bfloat16)
+    ex.fourth(0)
+    loads[3].wait()
+    loads[4].wait()
+
+    per_owner = heads // seq_parts
+
+    def summary_copy(head, slot):
+        return pltpu.make_async_remote_copy(
+            src_ref=summary_v.at[head],
+            dst_ref=theirs_v.at[slot],
+            send_sem=side_send.at[2],
+            recv_sem=side_recv.at[2],
+            device_id=beside,
+            device_id_type=MESH_ID,
+        )
+
+    inner = lax.broadcasted_iota(jnp.int32, (STEP_ROWS, HD), 0)
+    first_at = start + lax.rem(inner, LANES_OF_TIME) * steps + lax.div(inner, LANES_OF_TIME)
+
+    def head_step(head, carry):
+        ex.ready(head)
+
+        @pl.when(head + 3 < heads)
+        def _():
+            ex.second(head + 3)
+
+        @pl.when(head + 2 < heads)
+        def _():
+            ex.third(head + 2)
+
+        @pl.when(head + 4 < heads)
+        def _():
+            ex.first(head + 4)
+
+        columns = pl.ds(pl.multiple_of(head * HD, HD), HD)
+        w_block = w_buf[head].reshape(normed_v.shape[1], HD)
+        projected = jnp.dot(
+            normed_v[...], w_block, preferred_element_type=jnp.float32
+        ).astype(jnp.bfloat16)
+        xp_v[...] = projected.astype(jnp.float32)
+        row = lax.broadcasted_iota(jnp.int32, (HALO, rows_ext), 1)
+        wanted = length - (TAPS - 1) + lax.broadcasted_iota(jnp.int32, (HALO, rows_ext), 0) - 2
+        step = lax.div(row, LANES_OF_TIME) - (TAPS - 1)
+        at = start + lax.rem(row, LANES_OF_TIME) * steps + step
+        real = (step >= 0) & (step < steps) & (wanted < length) & (wanted >= length - (TAPS - 1))
+        picker = (real & (at == wanted)).astype(jnp.bfloat16)
+        picked = jnp.dot(picker, projected, preferred_element_type=jnp.float32)
+        conv_w = conv_ref[:, columns]
+        conv_sum = conv_w[0:1] * xp_v[0:local_len]
+        for offset in range(1, TAPS):
+            shift = offset * LANES_OF_TIME
+            conv_sum = conv_sum + conv_w[offset : offset + 1] * xp_v[shift : shift + local_len]
+        x_conv = conv_sum.astype(jnp.bfloat16)
+        xc_v[...] = x_conv.astype(jnp.float32)
+        ga_v[...] = jnp.dot(x_conv, wa_v[head], preferred_element_type=jnp.float32)
+        gi_v[...] = jnp.dot(x_conv, wi_v[head], preferred_element_type=jnp.float32)
+
+        @pl.when(head + 1 < heads)
+        def _():
+            ex.fourth(head + 1)
+
+        rate = -8.0 * jax.nn.softplus(-decay_ref[:, columns])
+
+        def block(i, carry):
+            state, rate_sum = carry
+            rows = pl.ds(pl.multiple_of(i * STEP_ROWS, STEP_ROWS), STEP_ROWS)
+            valid = first_at + i * (STEP_ROWS // LANES_OF_TIME) < length
+            log_rate = rate * jax.nn.sigmoid(ga_v[rows])
+            fall = -2.0 * log_rate
+            lost = 1.0 - fall * (1.0 / 6.0)
+            for order in (5.0, 4.0, 3.0, 2.0):
+                lost = 1.0 - fall * (1.0 / order) * lost
+            lost = fall * lost
+            root = lost * lax.rsqrt(jnp.maximum(lost, 1e-37))
+            push = jnp.where(valid, root * jax.nn.sigmoid(gi_v[rows]) * xc_v[rows], 0.0)
+            held = jnp.where(valid, log_rate, 0.0)
+            keep = jnp.exp(held)
+            for k in range(STEP_ROWS // LANES_OF_TIME):
+                tile = slice(k * LANES_OF_TIME, (k + 1) * LANES_OF_TIME)
+                state = keep[tile] * state + push[tile]
+                rate_sum = rate_sum + held[tile]
+            return state, rate_sum
+
+        zeros = jnp.zeros((LANES_OF_TIME, HD), jnp.float32)
+        state, rate_sum = lax.fori_loop(0, local_len // STEP_ROWS, block, (zeros, zeros))
+        keep_all = jnp.exp(rate_sum)
+        total = state[0:1]
+        for s in range(1, LANES_OF_TIME):
+            total = keep_all[s : s + 1] * total + state[s : s + 1]
+        keep_total = jnp.exp(jnp.sum(rate_sum, axis=0, keepdims=True))
+        place = lax.broadcasted_iota(jnp.int32, (LANES_OF_TIME, HD), 0)
+        summary_v[head] = jnp.where(
+            place == 0, keep_total, jnp.where(place == 1, total, picked[0:LANES_OF_TIME])
+        )
+
+        @pl.when(lax.div(head, per_owner) != y)
+        def _():
+            summary_copy(head, lax.rem(head, per_owner)).start()
+
+        ex.settled(head)
+        return carry
+
+    lax.fori_loop(0, heads, head_step, 0)
+
+    every = summary_v.at[pl.ds(0, per_owner)]
+    exchanged = pltpu.make_async_remote_copy(
+        src_ref=every,
+        dst_ref=theirs_v,
+        send_sem=side_send.at[2],
+        recv_sem=side_recv.at[2],
+        device_id=beside,
+        device_id_type=MESH_ID,
+    )
+    exchanged.wait_recv()
+    place = lax.broadcasted_iota(jnp.int32, (LANES_OF_TIME, HD), 0)
+    for k in range(per_owner):
+        own = summary_v[y * per_owner + k]
+        got = theirs_v[k]
+        head_part = jnp.where(y == 0, own, got)
+        tail_part = jnp.where(y == 0, got, own)
+        state = tail_part[0:1] * head_part[1:2] + tail_part[1:2]
+        state_ref[:, k * HD : (k + 1) * HD] = jnp.where(place == 0, state, head_part + tail_part)
+    exchanged.wait_send()
+
+    @pl.when(y == 0)
+    def _():
+        halo_copy.wait_send()
+
+    kv_copy.wait()
+    kept.wait()
+    blank.wait()
+
+
+def gathered_on_device(
+    sizes, tokens, attn_in, lengths, norm_gain, attn_gain, w_x, conv_w, w_a, w_i, lru_decay, w_kv
+):
+    local_len, width = tokens.shape[1:]
+    z_size, x_size, cores, seq_parts = sizes
+    heads = width // HD
+    rows_ext = -(-(local_len + (TAPS - 1) * LANES_OF_TIME) // HALO) * HALO
+    anywhere = pl.BlockSpec(memory_space=pl.ANY)
+    vmem = pl.BlockSpec(memory_space=pltpu.VMEM)
+    owned = width // seq_parts
+    per_owner = heads // seq_parts
+    half = w_kv.shape[1] // seq_parts
+    summary, cache = pl.pallas_call(
+        functools.partial(prefill_kernel, sizes),
+        in_specs=[
+            pl.BlockSpec(memory_space=pltpu.SMEM),
+            anywhere,
+            anywhere,
+            vmem,
+            vmem,
+            anywhere,
+            vmem,
+            anywhere,
+            anywhere,
+            vmem,
+            anywhere,
+        ],
+        out_specs=(vmem, anywhere),
+        out_shape=(
+            jax.ShapeDtypeStruct((LANES_OF_TIME, owned), jnp.float32),
+            jax.ShapeDtypeStruct((W, half), jnp.bfloat16),
+        ),
+        scratch_shapes=[
+            pltpu.VMEM((heads, z_size, x_size, cores, seq_parts, w_x.shape[0], HD), jnp.bfloat16),
+            pltpu.VMEM((local_len, width), jnp.bfloat16),
+            pltpu.VMEM((local_len, width), jnp.bfloat16),
+            pltpu.VMEM(w_kv.shape, jnp.bfloat16),
+            pltpu.VMEM(w_a.shape, jnp.bfloat16),
+            pltpu.VMEM(w_i.shape, jnp.bfloat16),
+            pltpu.VMEM((HALO, width), jnp.bfloat16),
+            pltpu.VMEM((local_len, width), jnp.bfloat16),
+            pltpu.VMEM((rows_ext, width), jnp.bfloat16),
+            pltpu.VMEM((2, local_len, half), jnp.bfloat16),
+            pltpu.VMEM((W - seq_parts * local_len, half), jnp.bfloat16),
+            pltpu.VMEM((rows_ext, HD), jnp.float32),
+            pltpu.VMEM((local_len, HD), jnp.float32),
+            pltpu.VMEM((local_len, HD), jnp.float32),
+            pltpu.VMEM((local_len, HD), jnp.float32),
+            pltpu.VMEM((heads, LANES_OF_TIME, HD), jnp.float32),
+            pltpu.VMEM((per_owner, LANES_OF_TIME, HD), jnp.float32),
+            pltpu.VMEM((2, local_len // 2, HD // 2), jnp.float32),
+            pltpu.SemaphoreType.DMA((heads, 3, 2)),
+            pltpu.SemaphoreType.DMA((heads, 3, 2)),
+            pltpu.SemaphoreType.DMA((heads,)),
+            pltpu.SemaphoreType.DMA((heads,)),
+            pltpu.SemaphoreType.DMA((heads + 7,)),
+            pltpu.SemaphoreType.DMA((3,)),
+            pltpu.SemaphoreType.DMA((3,)),
+        ],
+        compiler_params=pltpu.CompilerParams(
+            collective_id=0, has_side_effects=True, vmem_limit_bytes=60 * 1024 * 1024
+        ),
+    )(
+        lengths,
+        tokens[0],
+        attn_in[0],
+        norm_gain[None],
+        attn_gain[None],
+        w_x,
+        conv_w,
+        w_a,
+        w_i,
+        lru_decay[None],
+        w_kv,
+    )
+    return summary[0:1], summary[2 : 2 + TAPS - 1].astype(jnp.bfloat16)[None], cache[None]
+
+
+def fits(mesh, sizes, tokens, w_x, w_kv):
+    if sizes is None:
+        return False
+    _, length, width = tokens.shape
+    devices = mesh.size
+    seq_parts = mesh.shape["seq"]
+    return (
+        length < W
+        and width % (HD * seq_parts) == 0
+        and w_x.shape[0] % (devices * HALO) == 0
+        and w_x.shape[0] // devices > PLANE_ROWS + CROSS_ROWS
+        and w_kv.shape[1] == seq_parts * HD
+        and tokens.shape[0] == mesh.shape["batch"]
+    )
+
+
 def solution(mesh):
     in_specs = (
         P("batch", "seq", None),
@@ -255,6 +896,15 @@
         P(),
     )
     out_specs = (P("batch", "seq"), P("batch", None, "seq"), P("batch", None, "seq"))
-    return jax.shard_map(
-        on_device, mesh=mesh, in_specs=in_specs, out_specs=out_specs, check_vma=False
-    )
+    sizes = physical_grid(mesh)
+
+    def run(*arrays):
+        tokens, w_x, w_kv = arrays[0], arrays[5], arrays[10]
+        body = on_device
+        if fits(mesh, sizes, tokens, w_x, w_kv):
+            body = functools.partial(gathered_on_device, sizes)
+        return jax.shard_map(
+            body, mesh=mesh, in_specs=in_specs, out_specs=out_specs, check_vma=False
+        )(*arrays)
+
+    return run

time: 186 us -> 98.2 us (0.53)
  waiting for transfers between devices: 103 us -> 0 us
  Pallas kernels: 36.1 us -> 87.4 us
  between operations: 14.8 us -> 1.29 us
  starting transfers between devices: 8.48 us -> 0 us
  other arithmetic: 7.04 us -> 0 us
  blocking collectives: 5.22 us -> 0 us
    all_gather x2 -> x0, waiting for transfers between devices: 96.8 us -> none  [the longest x1 65.6 us: on_device(): lax.all_gather(w_x[:, :early * HD], ('batch', 'seq'), axis=0, tiled=True)]
    pallas_call x2 -> x1, Pallas kernels: 36.1 us -> 87.4 us  [gathered_on_device(): pl.pallas_call(functools.partial(prefill_kernel, sizes), in_specs=[pl.Blo...]
    all_to_all x1 -> x0, waiting for transfers between devices: 5.99 us -> none  [on_device(): lax.all_to_all(masked, 'seq', split_axis=1, concat_axis=0, tiled=True)]
    all_gather x1 -> x0, blocking collectives: 5.22 us -> none  [on_device(): gathered = lax.all_gather(summary, 'seq', axis=0, tiled=True)]
    all_to_all x1 -> x0, starting transfers between devices: 4.26 us -> none  [on_device(): lax.all_to_all(masked, 'seq', split_axis=1, concat_axis=0, tiled=True)]
    ppermute x1 -> x0, starting transfers between devices: 4.18 us -> none  [passed_along(): return lax.ppermute(block, axis, route)]
    broadcast_in_dim x2 -> x4, local copies, waits for them, and re-layouts: 1.21 us -> 5.33 us  [the longest x1 1.38 us: gathered_on_device(): summary[2:2 + TAPS - 1].astype(jnp.bfloat16)[None]]
    reduce_sum x1 -> x0, other arithmetic: 2.48 us -> none  [rms_norm(): jnp.mean(widened * widened, axis=-1, keepdims=True) + 1e-06]
  transfers between devices with their start and end apart: 4 -> 0, of which waited for: 3 -> 0; matrix products, arithmetic and copies ran while one was open for 6% -> 0% of each run, Pallas kernels for 14% -> 0%
where the time goes in v1:
time: 98.2 us; the launch traced here: 97.7 us
  Pallas kernels  87.4 us (89%)
  local copies, waits for them, and re-layouts  8.97 us (9%)
  between operations  1.29 us (1%)
    pallas_call x1, Pallas kernels, gathered_on_device(): pl.pallas_call(functools.partial(prefill_kernel, sizes), in_specs=[pl.Blo...  87.4 us
    unnamed x1, local copies, waits for them, and re-layouts  2.26 us

profile of v1, /device:TPU:0, one launch (start us, length us, event | category | flops | bytes accessed | tf_op | source)
XLA Modules:
  0.0 97.7 jit_solution(8383525045176984295)
XLA Ops:
  0.6 1.3 %broadcast_in_dim.15.norm_gain_ref = f32[1,2560]{1,0:T(1,128)} reshape(f32[2560]{0:T(1024)} %param.14) | data formatting | bytes 20480 | tf_op jit(solution)/shard_map/broadcast_in_dim | solution.py:856
  1.9 1.3 %broadcast_in_dim.16.attn_gain_ref = f32[1,2560]{1,0:T(1,128)} reshape(f32[2560]{0:T(1024)} %param.15) | data formatting | bytes 20480 | tf_op jit(solution)/shard_map/broadcast_in_dim | solution.py:857
  3.3 1.3 %broadcast_in_dim.17.decay_ref = f32[1,2560]{1,0:T(1,128)} reshape(f32[2560]{0:T(1024)} %param.20) | data formatting | bytes 20480 | tf_op jit(solution)/shard_map/broadcast_in_dim | solution.py:862
  5.2 87.4 %shard_map.130 = (f32[8,1280]{1,0:T(8,128)}, bf16[2048,256]{1,0:T(8,128)(2,1)}) custom-call(s32[1]{0:T(128)S(6)} %copy.15.length_ref, bf16[512,2560]{1,0:T(8,128)(2,1)} %bitcast.5, bf16[512,2560]{1,0:T(8,128)(2,1)} %bitcast.6, f32[1,2560]{1,0:T(1,128)} %broadcast_in_dim.15.norm_gain_ref, f32[1,2560]{1,0:T(1,128)} %broadcast_in_dim.16.attn_gain_ref, ...), custom_call_target="tpu_custom_call" | custom-call | tf_op jit(solution)/shard_map/pallas_call | solution.py:802
  92.6 1.4 %fusion = bf16[1,3,1280]{2,1,0:T(4,128)(2,1)} fusion(f32[8,1280]{1,0:T(8,128)} %get-tuple-element.5), kind=kLoop, calls=%fused_computation.1 | loop fusion | bytes 15360 | tf_op jit(solution)/shard_map/broadcast_in_dim | solution.py:865
  94.0 1.4 %slice.7 = f32[1,1280]{1,0:T(1,128)} slice(f32[8,1280]{1,0:T(8,128)} %get-tuple-element.5), slice={[0:1], [0:1280]} | slice | bytes 10240 | tf_op jit(solution)/shard_map/slice | solution.py:865
  95.4 2.3 %copy.16 = bf16[1,2048,256]{2,1,0:T(8,128)(2,1)} copy(bf16[1,2048,256]{2,1,0:T(8,128)(2,1)} %bitcast.7) | data formatting | bytes 2097152

commit v2 on v1

--- a/solution.py
+++ b/solution.py
@@ -242,7 +242,8 @@
 
 MESH_ID = pl.DeviceIdType.MESH
 PLANE_ROWS = 16
-CROSS_ROWS = 16
+WIDE_PLANE_ROWS = 32
+WIDE_HEADS = 2
 NEAR, PLANE = 0, 1
 
 
@@ -267,6 +268,32 @@
     return z_size, x_size, cores, y_size
 
 
+def scoped(method):
+    @functools.wraps(method)
+    def inside(*args):
+        with jax.named_scope(method.__name__):
+            return method(*args)
+
+    return inside
+
+
+def by_width(method):
+    @functools.wraps(method)
+    def inside(exchange, head):
+        border = exchange.heads - WIDE_HEADS
+        with jax.named_scope(method.__name__):
+            if isinstance(head, int):
+                method(exchange, head, PLANE_ROWS if head < border else WIDE_PLANE_ROWS)
+                return
+            for wide in (False, True):
+
+                @pl.when((head >= border) == wide)
+                def _():
+                    method(exchange, head, WIDE_PLANE_ROWS if wide else PLANE_ROWS)
+
+    return inside
+
+
 class Exchange:
     def __init__(self, sizes, heads, w_buf, send_sem, recv_sem, core_send, core_recv):
         self.sizes, self.heads = sizes, heads
@@ -279,7 +306,6 @@
         self.z = lax.div(at, cores * x_size)
         self.y = lax.axis_index("seq")
         self.shard_rows = w_buf.shape[5]
-        self.near_rows = self.shard_rows - PLANE_ROWS
         self.is_end = (self.z == 0) | (self.z == z_size - 1)
 
     def device(self, z=None, x=None, core=None, y=None):
@@ -304,12 +330,13 @@
         core = self.core if core is None else core
         return self.w_buf.at[head, z, x, core, y, pl.ds(first, rows)]
 
-    def copy(self, head, stage, group, part, to):
+    def copy(self, head, stage, group, plane_rows, part, to):
+        wide = 0 if plane_rows == PLANE_ROWS else 1
         return pltpu.make_async_remote_copy(
             src_ref=part,
             dst_ref=part,
-            send_sem=self.send_sem.at[head, stage, group],
-            recv_sem=self.recv_sem.at[head, stage, group],
+            send_sem=self.send_sem.at[stage, group, wide],
+            recv_sem=self.recv_sem.at[head, stage if group == NEAR or stage != 1 else 3],
             device_id=to,
             device_id_type=MESH_ID,
         )
@@ -318,7 +345,7 @@
         pltpu.make_async_remote_copy(
             src_ref=part,
             dst_ref=part,
-            send_sem=self.core_send.at[head],
+            send_sem=self.core_send.at[0],
             recv_sem=self.core_recv.at[head],
             device_id=self.device(core=1 - self.core),
             device_id_type=MESH_ID,
@@ -326,6 +353,8 @@
 
     def some(self, head, count, rows):
         every = slice(None)
+        if count == 2:
+            return self.w_buf.at[head, pl.ds(0, 2), 0, 0, 0, pl.ds(0, rows)]
         if count == 3:
             return self.w_buf.at[head, pl.ds(0, 3), 0, 0, 0, pl.ds(0, rows)]
         if count == 4:
@@ -335,56 +364,66 @@
         return self.w_buf.at[head, pl.ds(0, 3), every, 0, every, pl.ds(0, rows)]
 
     def arrived(self, head, stage, group, count, rows):
-        self.copy(head, stage, group, self.some(head, count, rows), self.device(core=1 - self.core)).wait_recv()
-
-    def left(self, head, stage, group, count, rows):
-        self.copy(head, stage, group, self.some(head, count, rows), self.device(core=1 - self.core)).wait_send()
-
-    def routes(self, act):
-        near = (PLANE_ROWS, self.near_rows)
+        part = self.some(head, count, rows)
+        self.copy(head, stage, group, PLANE_ROWS, part, self.device(core=1 - self.core)).wait_recv()
+
+    def left(self, stage, group, plane_rows, count, rows):
+        border = self.heads - WIDE_HEADS
+        span = pl.ds(0, border) if plane_rows == PLANE_ROWS else pl.ds(border, WIDE_HEADS)
+        part = self.some(span, count, rows)
+        self.copy(0, stage, group, plane_rows, part, self.device(core=1 - self.core)).wait_send()
+
+    def routes(self, plane_rows, act):
+        wide = WIDE_PLANE_ROWS
 
         @pl.when(self.core == 0)
         def _():
-            act("yx", PLANE_ROWS, CROSS_ROWS)
-            act("xy", PLANE_ROWS + CROSS_ROWS, self.near_rows - CROSS_ROWS)
+            if plane_rows < wide:
+                act("yx", plane_rows, wide - plane_rows)
+            act("xy", wide, self.shard_rows - wide)
 
         @pl.when(self.core != 0)
         def _():
-            act("yx", *near)
-
-    def first(self, head):
-        z_size = self.sizes[0]
-        near = self.blocks(head, self.z, self.x, self.y, PLANE_ROWS, self.near_rows)
-        for d in range(1, z_size):
-            self.copy(head, 0, NEAR, near, self.device(z=lax.rem(self.z + d, z_size))).start()
-        plane = self.blocks(head, self.z, self.x, self.y, 0, PLANE_ROWS)
-        self.copy(head, 0, PLANE, plane, self.device(x=1 - self.x)).start()
-        self.copy(head, 0, PLANE, plane, self.device(y=1 - self.y)).start()
-        self.copy(head, 0, PLANE, plane, self.device(x=1 - self.x, y=1 - self.y)).start()
-
-    def second(self, head):
+            act("yx", plane_rows, self.shard_rows - plane_rows)
+
+    @by_width
+    def first_near(self, head, plane_rows):
+        near = self.blocks(head, self.z, self.x, self.y, plane_rows, self.shard_rows - plane_rows)
+        for d in range(1, self.sizes[0]):
+            to = self.device(z=lax.rem(self.z + d, self.sizes[0]))
+            self.copy(head, 0, NEAR, plane_rows, near, to).start()
+
+    @by_width
+    def first_plane(self, head, plane_rows):
+        plane = self.blocks(head, self.z, self.x, self.y, 0, plane_rows)
+        self.copy(head, 0, PLANE, plane_rows, plane, self.device(x=1 - self.x)).start()
+        self.copy(head, 0, PLANE, plane_rows, plane, self.device(y=1 - self.y)).start()
+        self.copy(head, 0, PLANE, plane_rows, plane, self.device(x=1 - self.x, y=1 - self.y)).start()
+
+    @by_width
+    def second(self, head, plane_rows):
         every = slice(None)
         last = self.sizes[0] - 1
-        self.arrived(head, 0, NEAR, 3, self.near_rows)
+        self.arrived(head, 0, NEAR, 3, self.shard_rows)
 
         def near(order, first, rows):
             part = self.blocks(head, every, self.x, self.y, first, rows)
             to = self.device(x=1 - self.x) if order == "xy" else self.device(y=1 - self.y)
-            self.copy(head, 1, NEAR, part, to).start()
-
-        self.routes(near)
-        self.arrived(head, 0, PLANE, 3, PLANE_ROWS)
-        plane = self.blocks(head, self.z, every, every, 0, PLANE_ROWS)
+            self.copy(head, 1, NEAR, plane_rows, part, to).start()
+
+        self.routes(plane_rows, near)
+        plane = self.blocks(head, self.z, every, every, 0, plane_rows)
         up = jnp.where(self.z == last, 1, self.z + 1)
         down = jnp.where(self.z == 0, last - 1, self.z - 1)
-        self.copy(head, 1, PLANE, plane, self.device(z=up)).start()
-        self.copy(head, 1, PLANE, plane, self.device(z=down)).start()
+        self.copy(head, 1, PLANE, plane_rows, plane, self.device(z=up)).start()
+        self.copy(head, 1, PLANE, plane_rows, plane, self.device(z=down)).start()
         self.hand_over(head, plane)
 
-    def third(self, head):
+    @by_width
+    def third(self, head, plane_rows):
         every = slice(None)
         last = self.sizes[0] - 1
-        self.arrived(head, 1, NEAR, 4, self.near_rows)
+        self.arrived(head, 1, NEAR, 4, self.shard_rows - plane_rows)
 
         def near(order, first, rows):
             if order == "xy":
@@ -393,27 +432,35 @@
             else:
                 part = self.blocks(head, every, self.x, every, first, rows)
                 to = self.device(x=1 - self.x)
-            self.copy(head, 2, NEAR, part, to).start()
+            self.copy(head, 2, NEAR, plane_rows, part, to).start()
             self.hand_over(head, part)
 
-        self.routes(near)
+        self.routes(plane_rows, near)
 
         @pl.when(self.is_end)
         def _():
-            self.arrived(head, 1, PLANE, 4, PLANE_ROWS)
+            self.arrived(head, 1, PLANE, 4, plane_rows)
 
         @pl.when(jnp.logical_not(self.is_end))
         def _():
-            self.arrived(head, 1, PLANE, 12, PLANE_ROWS)
+            self.arrived(head, 1, PLANE, 12, plane_rows)
             half = (last + 1) // 2
             start = jnp.where(self.z >= half, 0, half)
-            part = self.blocks(head, pl.ds(start, half), every, every, 0, PLANE_ROWS)
-            self.copy(head, 2, PLANE, part, self.device(z=jnp.where(self.z >= half, last, 0))).start()
-
-    def fourth(self, head):
+            part = self.blocks(head, pl.ds(start, half), every, every, 0, plane_rows)
+            self.copy(head, 2, PLANE, plane_rows, part, self.device(z=jnp.where(self.z >= half, last, 0))).start()
+
+    @by_width
+    def fourth(self, head, plane_rows):
         every = slice(None)
         z_size = self.sizes[0]
-        self.arrived(head, 2, NEAR, 8, self.near_rows)
+
+        @pl.when(self.is_end)
+        def _():
+            self.arrived(head, 2, NEAR, 8, self.shard_rows)
+
+        @pl.when(jnp.logical_not(self.is_end))
+        def _():
+            self.arrived(head, 2, NEAR, 8, self.shard_rows - plane_rows)
 
         def near(order, first, rows):
             if order == "xy":
@@ -422,58 +469,58 @@
                 part = self.blocks(head, every, 1 - self.x, every, first, rows)
             self.hand_over(head, part)
 
-        self.routes(near)
-
-        @pl.when(self.is_end)
-        def _():
-            self.arrived(head, 2, PLANE, 8, PLANE_ROWS)
+        self.routes(plane_rows, near)
 
         for d in range(1, z_size):
-            self.hand_over(head, self.blocks(head, lax.rem(self.z + d, z_size), every, every, 0, PLANE_ROWS))
+            self.hand_over(head, self.blocks(head, lax.rem(self.z + d, z_size), every, every, 0, plane_rows))
 
     def handed(self, head, core):
-        every = slice(None)
-        part = self.w_buf.at[head, every, every, core]
+        part = self.w_buf.at[head, slice(None), slice(None), core]
         return pltpu.make_async_remote_copy(
             src_ref=part,
             dst_ref=part,
-            send_sem=self.core_send.at[head],
-            recv_sem=self.core_recv.at[head],
+            send_sem=self.core_send.at[0],
+            recv_sem=self.core_recv.at[0 if isinstance(head, slice) else head],
             device_id=self.device(core=1 - self.core),
             device_id_type=MESH_ID,
         )
 
+    @scoped
     def ready(self, head):
         self.handed(head, 1 - self.core).wait_recv()
 
-    def settled(self, head):
-        self.left(head, 0, NEAR, 3, self.near_rows)
-        self.left(head, 0, PLANE, 3, PLANE_ROWS)
-        self.left(head, 1, NEAR, 4, self.near_rows)
-        self.left(head, 1, PLANE, 8, PLANE_ROWS)
-        self.left(head, 2, NEAR, 8, self.near_rows)
-
-        @pl.when(jnp.logical_not(self.is_end))
-        def _():
-            self.left(head, 2, PLANE, 8, PLANE_ROWS)
-
-        self.handed(head, self.core).wait_send()
+    @scoped
+    def settled(self):
+        for plane_rows in (PLANE_ROWS, WIDE_PLANE_ROWS):
+            near_rows = self.shard_rows - plane_rows
+            self.left(0, NEAR, plane_rows, 3, near_rows)
+            self.left(0, PLANE, plane_rows, 3, plane_rows)
+            self.left(1, NEAR, plane_rows, 4, near_rows)
+            self.left(1, PLANE, plane_rows, 8, plane_rows)
+            self.left(2, NEAR, plane_rows, 8, near_rows)
+
+            @pl.when(jnp.logical_not(self.is_end))
+            def _():
+                self.left(2, PLANE, plane_rows, 8, plane_rows)
+
+        self.handed(slice(None), self.core).wait_send()
 
 
 def prefill_kernel(
     sizes,
-    length_ref,
+    length_hbm,
     tokens_hbm,
     attn_hbm,
-    norm_gain_ref,
-    attn_gain_ref,
+    norm_gain_hbm,
+    attn_gain_hbm,
     w_hbm,
-    conv_ref,
+    conv_hbm,
     wa_hbm,
     wi_hbm,
-    decay_ref,
+    decay_hbm,
     wkv_hbm,
-    state_ref,
+    own_ref,
+    theirs_ref,
     cache_ref,
     w_buf,
     tokens_v,
@@ -485,14 +532,17 @@
     rows_v,
     normed_v,
     kv_v,
-    zeros_v,
     xp_v,
     xc_v,
     ga_v,
     gi_v,
     summary_v,
-    theirs_v,
     turn_v,
+    norm_gain_ref,
+    attn_gain_ref,
+    decay_ref,
+    conv_ref,
+    length_ref,
     send_sem,
     recv_sem,
     core_send,
@@ -511,12 +561,12 @@
 
     shard = [
         pltpu.make_async_copy(
-            w_hbm.at[:, pl.ds(h * HD, HD)], w_buf.at[h, ex.z, ex.x, ex.core, y], load_sem.at[h]
+            w_hbm.at[:, pl.ds(h * HD, HD)], w_buf.at[h, ex.z, ex.x, ex.core, y], load_sem.at[12]
         )
         for h in range(heads)
     ]
     loads = [
-        pltpu.make_async_copy(source, target, load_sem.at[heads + i])
+        pltpu.make_async_copy(source, target, load_sem.at[i])
         for i, (source, target) in enumerate(
             (
                 (tokens_hbm, tokens_v),
@@ -524,10 +574,15 @@
                 (wkv_hbm, wkv_v),
                 (wa_hbm, wa_v),
                 (wi_hbm, wi_v),
+                (norm_gain_hbm, norm_gain_ref.at[0]),
+                (attn_gain_hbm, attn_gain_ref.at[0]),
+                (decay_hbm, decay_ref.at[0]),
+                (conv_hbm, conv_ref),
+                (length_hbm, length_ref),
             )
         )
     ]
-    for copy in shard + [loads[1], loads[2], loads[0], loads[3], loads[4]]:
+    for copy in shard + [loads[1], loads[2], loads[6], loads[9], loads[0], *loads[3:6], loads[7], loads[8]]:
         copy.start()
 
     barrier = pltpu.get_barrier_semaphore()
@@ -535,7 +590,15 @@
     for peer in peers:
         pl.semaphore_signal(barrier, inc=1, device_id=peer, device_id_type=MESH_ID)
 
-    zeros_v[...] = jnp.zeros_like(zeros_v)
+    own_shard = w_buf.at[:, ex.z, ex.x, ex.core, y]
+    pltpu.make_async_copy(own_shard, own_shard, load_sem.at[12]).wait()
+    pl.semaphore_wait(barrier, len(peers))
+    ex.first_near(0)
+    for h in range(heads):
+        ex.first_plane(h)
+    ex.first_near(1)
+    ex.first_near(2)
+
     quarter = HD // 4
     lane = lax.broadcasted_iota(jnp.int32, (1, 2 * quarter), 1)
     spacing = jnp.exp(
@@ -546,12 +609,8 @@
     turn_v[0] = jnp.cos(fine)
     turn_v[1] = jnp.sin(fine)
 
-    for copy in shard:
-        copy.wait()
-    pl.semaphore_wait(barrier, len(peers))
-    for h in range(4):
-        ex.first(h)
-
+    loads[6].wait()
+    loads[9].wait()
     length = length_ref[0]
 
     def kv_half(k):
@@ -585,36 +644,39 @@
         device_id=beside,
         device_id_type=MESH_ID,
     )
+    kv_copies = [
+        pltpu.make_async_remote_copy(
+            src_ref=kv_v.at[1 - y, pl.ds(k * half_len, half_len)],
+            dst_ref=cache_ref.at[pl.ds(start + k * half_len, half_len)],
+            send_sem=side_send.at[1 + k],
+            recv_sem=side_recv.at[1 + k],
+            device_id=beside,
+            device_id_type=MESH_ID,
+        )
+        for k in range(2)
+    ]
+    kept = pltpu.make_async_copy(kv_v.at[y], cache_ref.at[pl.ds(start, local_len)], load_sem.at[10])
     loads[1].wait()
     loads[2].wait()
-    kv_half(0)
-    ex.second(0)
+    with jax.named_scope("kv"):
+        kv_half(0)
     loads[0].wait()
+    loads[5].wait()
 
     @pl.when(y == 0)
     def _():
         halo_copy.start()
         halo_v[...] = jnp.zeros_like(halo_v)
 
-    kv_half(1)
+    ex.second(0)
+    kv_copies[0].start()
+    with jax.named_scope("kv"):
+        kv_half(1)
+    ex.second(1)
     ex.third(0)
-    ex.second(1)
-    kv_copy = pltpu.make_async_remote_copy(
-        src_ref=kv_v.at[1 - y],
-        dst_ref=cache_ref.at[pl.ds(start, local_len)],
-        send_sem=side_send.at[1],
-        recv_sem=side_recv.at[1],
-        device_id=beside,
-        device_id_type=MESH_ID,
-    )
-    kv_copy.start()
-    kept = pltpu.make_async_copy(kv_v.at[y], cache_ref.at[pl.ds(start, local_len)], load_sem.at[heads + 5])
+    ex.first_near(3)
+    kv_copies[1].start()
     kept.start()
-    rest = seq_parts * local_len
-    blank = pltpu.make_async_copy(
-        zeros_v, cache_ref.at[pl.ds(rest, cache_ref.shape[0] - rest)], load_sem.at[heads + 6]
-    )
-    blank.start()
 
     norm_step = 64
 
@@ -623,9 +685,11 @@
         rows_v[rows] = rms_norm(tokens_v[rows], norm_gain_ref[...])
         return carry
 
-    lax.fori_loop(0, local_len // norm_step, norm_rows, 0)
+    with jax.named_scope("norm"):
+        lax.fori_loop(0, local_len // norm_step, norm_rows, 0)
     ex.second(2)
     ex.third(1)
+    ex.first_near(4)
 
     @pl.when(y != 0)
     def _():
@@ -654,18 +718,19 @@
     halo_rows = rms_norm(halo_v[...], norm_gain_ref[...])
     before = jnp.dot(early, halo_rows, preferred_element_type=jnp.float32)
     normed_v[0:edge] = (normed_v[0:edge].astype(jnp.float32) + before).astype(jnp.bfloat16)
+    ex.second(3)
     ex.fourth(0)
-    loads[3].wait()
-    loads[4].wait()
+    for copy in (loads[3], loads[4], loads[7], loads[8]):
+        copy.wait()
 
     per_owner = heads // seq_parts
 
     def summary_copy(head, slot):
         return pltpu.make_async_remote_copy(
             src_ref=summary_v.at[head],
-            dst_ref=theirs_v.at[slot],
-            send_sem=side_send.at[2],
-            recv_sem=side_recv.at[2],
+            dst_ref=theirs_ref.at[slot],
+            send_sem=side_send.at[3],
+            recv_sem=side_recv.at[3],
             device_id=beside,
             device_id_type=MESH_ID,
         )
@@ -676,17 +741,11 @@
     def head_step(head, carry):
         ex.ready(head)
 
-        @pl.when(head + 3 < heads)
-        def _():
-            ex.second(head + 3)
-
-        @pl.when(head + 2 < heads)
-        def _():
-            ex.third(head + 2)
-
-        @pl.when(head + 4 < heads)
-        def _():
-            ex.first(head + 4)
+        for lag, stage in ((5, ex.first_near), (4, ex.second), (2, ex.third)):
+
+            @pl.when(head + lag < heads)
+            def _():
+                stage(head + lag)
 
         columns = pl.ds(pl.multiple_of(head * HD, HD), HD)
         w_block = w_buf[head].reshape(normed_v.shape[1], HD)
@@ -753,38 +812,84 @@
         def _():
             summary_copy(head, lax.rem(head, per_owner)).start()
 
-        ex.settled(head)
         return carry
 
     lax.fori_loop(0, heads, head_step, 0)
 
+    own = pltpu.make_async_copy(
+        summary_v.at[pl.ds(y * per_owner, per_owner)], own_ref, load_sem.at[11]
+    )
+    own.start()
     every = summary_v.at[pl.ds(0, per_owner)]
     exchanged = pltpu.make_async_remote_copy(
         src_ref=every,
-        dst_ref=theirs_v,
-        send_sem=side_send.at[2],
-        recv_sem=side_recv.at[2],
+        dst_ref=theirs_ref,
+        send_sem=side_send.at[3],
+        recv_sem=side_recv.at[3],
         device_id=beside,
         device_id_type=MESH_ID,
     )
-    exchanged.wait_recv()
-    place = lax.broadcasted_iota(jnp.int32, (LANES_OF_TIME, HD), 0)
-    for k in range(per_owner):
-        own = summary_v[y * per_owner + k]
-        got = theirs_v[k]
-        head_part = jnp.where(y == 0, own, got)
-        tail_part = jnp.where(y == 0, got, own)
-        state = tail_part[0:1] * head_part[1:2] + tail_part[1:2]
-        state_ref[:, k * HD : (k + 1) * HD] = jnp.where(place == 0, state, head_part + tail_part)
-    exchanged.wait_send()
+    for copy in kv_copies:
+        copy.wait()
+    kept.wait()
 
     @pl.when(y == 0)
     def _():
         halo_copy.wait_send()
 
-    kv_copy.wait()
-    kept.wait()
-    blank.wait()
+    ex.settled()
+    with jax.named_scope("exchanged"):
+        own.wait()
+        exchanged.wait()
+
+
+def finish_kernel(
+    own_hbm,
+    theirs_hbm,
+    kv_hbm,
+    state_hbm,
+    conv_hbm,
+    cache_hbm,
+    zeros_v,
+    kv_v,
+    own_v,
+    theirs_v,
+    state_v,
+    conv_v,
+    in_sem,
+    out_sem,
+):
+    rest = kv_v.shape[0]
+    load_own = pltpu.make_async_copy(own_hbm, own_v, in_sem.at[0])
+    load_theirs = pltpu.make_async_copy(theirs_hbm, theirs_v, in_sem.at[1])
+    load_kv = pltpu.make_async_copy(kv_hbm, kv_v, in_sem.at[2])
+    for copy in (load_own, load_theirs, load_kv):
+        copy.start()
+    zeros_v[...] = jnp.zeros_like(zeros_v)
+    store = [
+        pltpu.make_async_copy(zeros_v, cache_hbm.at[pl.ds(rest, zeros_v.shape[0])], out_sem.at[0]),
+        pltpu.make_async_copy(kv_v, cache_hbm.at[pl.ds(0, rest)], out_sem.at[1]),
+        pltpu.make_async_copy(state_v, state_hbm, out_sem.at[2]),
+        pltpu.make_async_copy(conv_v, conv_hbm, out_sem.at[3]),
+    ]
+    store[0].start()
+    load_own.wait()
+    load_theirs.wait()
+    first_half = lax.axis_index("seq") == 0
+    for k in range(own_v.shape[0]):
+        own, got = own_v[k], theirs_v[k]
+        head_part = jnp.where(first_half, own, got)
+        tail_part = jnp.where(first_half, got, own)
+        columns = slice(k * HD, (k + 1) * HD)
+        state_v[:, columns] = tail_part[0:1] * head_part[1:2] + tail_part[1:2]
+        picked = head_part[2 : 1 + TAPS] + tail_part[2 : 1 + TAPS]
+        conv_v[0, :, columns] = picked.astype(jnp.bfloat16)
+    store[2].start()
+    store[3].start()
+    load_kv.wait()
+    store[1].start()
+    for copy in store:
+        copy.wait()
 
 
 def gathered_on_device(
@@ -795,29 +900,17 @@
     heads = width // HD
     rows_ext = -(-(local_len + (TAPS - 1) * LANES_OF_TIME) // HALO) * HALO
     anywhere = pl.BlockSpec(memory_space=pl.ANY)
-    vmem = pl.BlockSpec(memory_space=pltpu.VMEM)
     owned = width // seq_parts
     per_owner = heads // seq_parts
     half = w_kv.shape[1] // seq_parts
-    summary, cache = pl.pallas_call(
+    own, theirs, kv = pl.pallas_call(
         functools.partial(prefill_kernel, sizes),
-        in_specs=[
-            pl.BlockSpec(memory_space=pltpu.SMEM),
-            anywhere,
-            anywhere,
-            vmem,
-            vmem,
-            anywhere,
-            vmem,
-            anywhere,
-            anywhere,
-            vmem,
-            anywhere,
-        ],
-        out_specs=(vmem, anywhere),
+        in_specs=[anywhere] * 11,
+        out_specs=(anywhere, anywhere, anywhere),
         out_shape=(
-            jax.ShapeDtypeStruct((LANES_OF_TIME, owned), jnp.float32),
-            jax.ShapeDtypeStruct((W, half), jnp.bfloat16),
+            jax.ShapeDtypeStruct((per_owner, LANES_OF_TIME, HD), jnp.float32),
+            jax.ShapeDtypeStruct((per_owner, LANES_OF_TIME, HD), jnp.float32),
+            jax.ShapeDtypeStruct((seq_parts * local_len, half), jnp.bfloat16),
         ),
         scratch_shapes=[
             pltpu.VMEM((heads, z_size, x_size, cores, seq_parts, w_x.shape[0], HD), jnp.bfloat16),
@@ -830,21 +923,24 @@
             pltpu.VMEM((local_len, width), jnp.bfloat16),
             pltpu.VMEM((rows_ext, width), jnp.bfloat16),
             pltpu.VMEM((2, local_len, half), jnp.bfloat16),
-            pltpu.VMEM((W - seq_parts * local_len, half), jnp.bfloat16),
             pltpu.VMEM((rows_ext, HD), jnp.float32),
             pltpu.VMEM((local_len, HD), jnp.float32),
             pltpu.VMEM((local_len, HD), jnp.float32),
             pltpu.VMEM((local_len, HD), jnp.float32),
             pltpu.VMEM((heads, LANES_OF_TIME, HD), jnp.float32),
-            pltpu.VMEM((per_owner, LANES_OF_TIME, HD), jnp.float32),
             pltpu.VMEM((2, local_len // 2, HD // 2), jnp.float32),
-            pltpu.SemaphoreType.DMA((heads, 3, 2)),
-            pltpu.SemaphoreType.DMA((heads, 3, 2)),
+            pltpu.VMEM((1, width), jnp.float32),
+            pltpu.VMEM((1, width), jnp.float32),
+            pltpu.VMEM((1, width), jnp.float32),
+            pltpu.VMEM(conv_w.shape, jnp.float32),
+            pltpu.SMEM((1,), jnp.int32),
+            pltpu.SemaphoreType.DMA((3, 2, 2)),
+            pltpu.SemaphoreType.DMA((heads, 4)),
+            pltpu.SemaphoreType.DMA((1,)),
             pltpu.SemaphoreType.DMA((heads,)),
-            pltpu.SemaphoreType.DMA((heads,)),
-            pltpu.SemaphoreType.DMA((heads + 7,)),
-            pltpu.SemaphoreType.DMA((3,)),
-            pltpu.SemaphoreType.DMA((3,)),
+            pltpu.SemaphoreType.DMA((13,)),
+            pltpu.SemaphoreType.DMA((4,)),
+            pltpu.SemaphoreType.DMA((4,)),
         ],
         compiler_params=pltpu.CompilerParams(
             collective_id=0, has_side_effects=True, vmem_limit_bytes=60 * 1024 * 1024
@@ -853,16 +949,37 @@
         lengths,
         tokens[0],
         attn_in[0],
-        norm_gain[None],
-        attn_gain[None],
+        norm_gain,
+        attn_gain,
         w_x,
         conv_w,
         w_a,
         w_i,
-        lru_decay[None],
+        lru_decay,
         w_kv,
     )
-    return summary[0:1], summary[2 : 2 + TAPS - 1].astype(jnp.bfloat16)[None], cache[None]
+    state_shape, conv_shape = (1, owned), (1, TAPS - 1, owned)
+    state, conv_state, cache = pl.pallas_call(
+        finish_kernel,
+        in_specs=[anywhere] * 3,
+        out_specs=(anywhere, anywhere, anywhere),
+        out_shape=(
+            jax.ShapeDtypeStruct(state_shape, jnp.float32),
+            jax.ShapeDtypeStruct(conv_shape, jnp.bfloat16),
+            jax.ShapeDtypeStruct((W, half), jnp.bfloat16),
+        ),
+        scratch_shapes=[
+            pltpu.VMEM((W - kv.shape[0], half), jnp.bfloat16),
+            pltpu.VMEM(kv.shape, jnp.bfloat16),
+            pltpu.VMEM(own.shape, jnp.float32),
+            pltpu.VMEM(own.shape, jnp.float32),
+            pltpu.VMEM(state_shape, jnp.float32),
+            pltpu.VMEM(conv_shape, jnp.bfloat16),
+            pltpu.SemaphoreType.DMA((3,)),
+            pltpu.SemaphoreType.DMA((4,)),
+        ],
+    )(own, theirs, kv)
+    return state, conv_state, cache[None]
 
 
 def fits(mesh, sizes, tokens, w_x, w_kv):
@@ -875,7 +992,7 @@
         length < W
         and width % (HD * seq_parts) == 0
         and w_x.shape[0] % (devices * HALO) == 0
-        and w_x.shape[0] // devices > PLANE_ROWS + CROSS_ROWS
+        and w_x.shape[0] // devices > WIDE_PLANE_ROWS
         and w_kv.shape[1] == seq_parts * HD
         and tokens.shape[0] == mesh.shape["batch"]
     )

time: 98.2 us -> 71.6 us (0.73)
  Pallas kernels: 87.4 us -> 70.2 us
  local copies, waits for them, and re-layouts: 8.97 us -> 0 us
    pallas_call x1 -> x2, Pallas kernels: 87.4 us -> 70.2 us  [the longest x1 68 us: gathered_on_device(): pl.pallas_call(functools.partial(prefill_kernel, sizes), in_specs=[anywhe...]
    broadcast_in_dim x4 -> x0, local copies, waits for them, and re-layouts: 5.33 us -> none  [the longest x1 1.38 us: gathered_on_device(): summary[2:2 + TAPS - 1].astype(jnp.bfloat16)[None]]
    unnamed x1 -> x0, local copies, waits for them, and re-layouts: 2.26 us -> none
    slice x1 -> x0, local copies, waits for them, and re-layouts: 1.37 us -> none  [gathered_on_device(): summary[0:1]]
where the time goes in v2:
time: 71.6 us; the launch traced here: 71.5 us
  Pallas kernels  70.2 us (98%)
  between operations  1.29 us (2%)
    pallas_call x1, Pallas kernels, gathered_on_device(): pl.pallas_call(functools.partial(prefill_kernel, sizes), in_specs=[anywhe...  68 us
    pallas_call x1, Pallas kernels, gathered_on_device(): pl.pallas_call(finish_kernel, in_specs=[anywhere] * 3, out_specs=(anywher...  2.14 us

profile of v2, /device:TPU:0, one launch (start us, length us, event | category | flops | bytes accessed | tf_op | source)
XLA Modules:
  0.0 71.5 jit_solution(17837508976932978135)
XLA Ops:
  1.3 68.0 %shard_map.130 = (f32[5,8,256]{2,1,0:T(8,128)}, f32[5,8,256]{2,1,0:T(8,128)}, bf16[1024,256]{1,0:T(8,128)(2,1)}) custom-call(s32[1]{0:T(128)S(6)} %copy.14.length_hbm, bf16[512,2560]{1,0:T(8,128)(2,1)} %bitcast.3, bf16[512,2560]{1,0:T(8,128)(2,1)} %bitcast.4, f32[2560]{0:T(1024)} %norm_gain_hbm.1, f32[2560]{0:T(1024)} %attn_gain_hbm.1, ...), custom_call_target="tpu_custom_call" | custom-call | tf_op jit(solution)/shard_map/pallas_call | solution.py:906
  69.3 2.1 %shard_map.131 = (f32[1,1280]{1,0:T(1,128)}, bf16[1,3,1280]{2,1,0:T(4,128)(2,1)}, bf16[2048,256]{1,0:T(8,128)(2,1)}) custom-call(f32[5,8,256]{2,1,0:T(8,128)} %get-tuple-element.9.own_hbm, f32[5,8,256]{2,1,0:T(8,128)} %get-tuple-element.10.theirs_hbm, bf16[1024,256]{1,0:T(8,128)(2,1)} %get-tuple-element.11.kv_hbm), custom_call_target="tpu_custom_call" | custom-call | tf_op jit(solution)/shard_map/pallas_call | solution.py:962

commit v3 on v2

--- a/solution.py
+++ b/solution.py
@@ -241,10 +241,91 @@
 
 
 MESH_ID = pl.DeviceIdType.MESH
-PLANE_ROWS = 16
-WIDE_PLANE_ROWS = 32
-WIDE_HEADS = 2
+SPLITS = ((6, (16, 16)), (4, (16, 0)),)
 NEAR, PLANE = 0, 1
+START = (
+    ("plane", 0), ("near", 1), ("own", 0), ("own", 4), ("own", 1), ("plane", 1), ("near", 0), ("plane", 2),
+    ("own", 3), ("kv", 0), ("halo", 0), ("send_kv", 0), ("own", 2), ("plane", 3), ("near", 2), ("kv", 1),
+    ("second", 0), ("near", 3), ("norm", 0), ("second", 1), ("plane", 4), ("third_plane", 0), ("second", 2),
+    ("reorder", 0), ("near", 4), ("third", 0), ("second", 3), ("send_kv", 1), ("third", 1), ("third_plane", 1),
+    ("plane", 6), ("reorder", 1),
+)
+SLOTS = (
+    (
+        (
+            ("plane", 5), ("plane", 7), ("fourth", 0), ("third", 2), ("third", 3), ("third_plane", 2), ("near", 5),
+            ("own", 7), ("own", 5), ("second", 4), ("fourth", 1), ("ready", 0),
+        ),
+        (),
+    ),
+    (
+        (
+            ("own", 6), ("plane", 8), ("third_plane", 3), ("near", 6), ("second", 5), ("fourth", 2), ("ready", 1),
+        ),
+        (
+            ("plane", 9), ("third", 4),
+        ),
+    ),
+    (
+        (
+            ("near", 7), ("third_plane", 4), ("second", 6), ("third", 5), ("ready", 2), ("fourth", 3),
+        ),
+        (),
+    ),
+    (
+        (
+            ("own", 8), ("near", 8), ("third_plane", 5), ("third_plane", 6), ("second", 7), ("ready", 3),
+            ("third", 6),
+        ),
+        (
+            ("fourth", 4), ("own", 9),
+        ),
+    ),
+    (
+        (
+            ("near", 9), ("third", 7), ("second", 8), ("ready", 4),
+        ),
+        (
+            ("fourth", 5),
+        ),
+    ),
+    (
+        (
+            ("third_plane", 7), ("fourth", 6), ("ready", 5), ("second", 9),
+        ),
+        (
+            ("third", 8),
+        ),
+    ),
+    (
+        (
+            ("fourth", 7), ("ready", 6), ("third_plane", 8),
+        ),
+        (
+            ("third", 9),
+        ),
+    ),
+    (
+        (
+            ("third_plane", 9), ("ready", 7),
+        ),
+        (
+            ("fourth", 8),
+        ),
+    ),
+    (
+        (
+            ("ready", 8), ("fourth", 9),
+        ),
+        (),
+    ),
+    (
+        (
+            ("ready", 9),
+        ),
+        (),
+    ),
+)
 
 
 def physical_grid(mesh):
@@ -277,19 +358,25 @@
     return inside
 
 
-def by_width(method):
+def by_split(method):
     @functools.wraps(method)
     def inside(exchange, head):
-        border = exchange.heads - WIDE_HEADS
         with jax.named_scope(method.__name__):
-            if isinstance(head, int):
-                method(exchange, head, PLANE_ROWS if head < border else WIDE_PLANE_ROWS)
-                return
-            for wide in (False, True):
-
-                @pl.when((head >= border) == wide)
-                def _():
-                    method(exchange, head, WIDE_PLANE_ROWS if wide else PLANE_ROWS)
+            first = 0
+            for index, (count, _) in enumerate(SPLITS):
+                last = first + count
+                if isinstance(head, int):
+                    if first <= head < last:
+                        method(exchange, head, index)
+                elif len(SPLITS) == 1:
+                    method(exchange, head, index)
+                else:
+
+                    @pl.when((head >= first) & (head < last))
+                    def _():
+                        method(exchange, head, index)
+
+                first = last
 
     return inside
 
@@ -330,12 +417,11 @@
         core = self.core if core is None else core
         return self.w_buf.at[head, z, x, core, y, pl.ds(first, rows)]
 
-    def copy(self, head, stage, group, plane_rows, part, to):
-        wide = 0 if plane_rows == PLANE_ROWS else 1
+    def copy(self, head, stage, group, split, part, to):
         return pltpu.make_async_remote_copy(
             src_ref=part,
             dst_ref=part,
-            send_sem=self.send_sem.at[stage, group, wide],
+            send_sem=self.send_sem.at[stage, group, split],
             recv_sem=self.recv_sem.at[head, stage if group == NEAR or stage != 1 else 3],
             device_id=to,
             device_id_type=MESH_ID,
@@ -365,77 +451,100 @@
 
     def arrived(self, head, stage, group, count, rows):
         part = self.some(head, count, rows)
-        self.copy(head, stage, group, PLANE_ROWS, part, self.device(core=1 - self.core)).wait_recv()
-
-    def left(self, stage, group, plane_rows, count, rows):
-        border = self.heads - WIDE_HEADS
-        span = pl.ds(0, border) if plane_rows == PLANE_ROWS else pl.ds(border, WIDE_HEADS)
-        part = self.some(span, count, rows)
-        self.copy(0, stage, group, plane_rows, part, self.device(core=1 - self.core)).wait_send()
-
-    def routes(self, plane_rows, act):
-        wide = WIDE_PLANE_ROWS
+        self.copy(head, stage, group, 0, part, self.device(core=1 - self.core)).wait_recv()
+
+    def left(self, stage, group, split, count, rows):
+        first = sum(n for n, _ in SPLITS[:split])
+        part = self.some(pl.ds(first, SPLITS[split][0]), count, rows)
+        self.copy(0, stage, group, split, part, self.device(core=1 - self.core)).wait_send()
+
+    def routes(self, split, act):
+        plane_rows, turned = SPLITS[split][1]
 
         @pl.when(self.core == 0)
         def _():
-            if plane_rows < wide:
-                act("yx", plane_rows, wide - plane_rows)
-            act("xy", wide, self.shard_rows - wide)
+            if turned:
+                act("yx", plane_rows, turned)
+            act("xy", plane_rows + turned, self.shard_rows - plane_rows - turned)
 
         @pl.when(self.core != 0)
         def _():
             act("yx", plane_rows, self.shard_rows - plane_rows)
 
-    @by_width
-    def first_near(self, head, plane_rows):
-        near = self.blocks(head, self.z, self.x, self.y, plane_rows, self.shard_rows - plane_rows)
+    @by_split
+    def near(self, head, split):
+        plane_rows = SPLITS[split][1][0]
+        part = self.blocks(head, self.z, self.x, self.y, plane_rows, self.shard_rows - plane_rows)
         for d in range(1, self.sizes[0]):
             to = self.device(z=lax.rem(self.z + d, self.sizes[0]))
-            self.copy(head, 0, NEAR, plane_rows, near, to).start()
-
-    @by_width
-    def first_plane(self, head, plane_rows):
+            self.copy(head, 0, NEAR, split, part, to).start()
+
+    def across(self, order):
+        beside = self.device(x=1 - self.x), self.device(y=1 - self.y)
+        return beside if order == "xy" else beside[::-1]
+
+    @by_split
+    def own(self, head, split):
+        def near(order, first, rows):
+            own = self.blocks(head, self.z, self.x, self.y, first, rows)
+            for stage, to in enumerate(self.across(order)):
+                self.copy(head, 1 + stage, NEAR, split, own, to).start()
+
+        self.routes(split, near)
+
+    @by_split
+    def plane(self, head, split):
+        plane_rows = SPLITS[split][1][0]
         plane = self.blocks(head, self.z, self.x, self.y, 0, plane_rows)
-        self.copy(head, 0, PLANE, plane_rows, plane, self.device(x=1 - self.x)).start()
-        self.copy(head, 0, PLANE, plane_rows, plane, self.device(y=1 - self.y)).start()
-        self.copy(head, 0, PLANE, plane_rows, plane, self.device(x=1 - self.x, y=1 - self.y)).start()
-
-    @by_width
-    def second(self, head, plane_rows):
+        self.copy(head, 0, PLANE, split, plane, self.device(x=1 - self.x)).start()
+        self.copy(head, 0, PLANE, split, plane, self.device(y=1 - self.y)).start()
+        self.copy(head, 0, PLANE, split, plane, self.device(x=1 - self.x, y=1 - self.y)).start()
+
+    @by_split
+    def second(self, head, split):
+        plane_rows = SPLITS[split][1][0]
         every = slice(None)
         last = self.sizes[0] - 1
         self.arrived(head, 0, NEAR, 3, self.shard_rows)
 
         def near(order, first, rows):
-            part = self.blocks(head, every, self.x, self.y, first, rows)
-            to = self.device(x=1 - self.x) if order == "xy" else self.device(y=1 - self.y)
-            self.copy(head, 1, NEAR, plane_rows, part, to).start()
-
-        self.routes(plane_rows, near)
+            for stage, to in enumerate(self.across(order)):
+                for d in range(1, last + 1):
+                    at = lax.rem(self.z + d, last + 1)
+                    part = self.blocks(head, at, self.x, self.y, first, rows)
+                    self.copy(head, 1 + stage, NEAR, split, part, to).start()
+            self.hand_over(head, self.blocks(head, every, self.x, self.y, first, rows))
+
+        self.routes(split, near)
         plane = self.blocks(head, self.z, every, every, 0, plane_rows)
         up = jnp.where(self.z == last, 1, self.z + 1)
         down = jnp.where(self.z == 0, last - 1, self.z - 1)
-        self.copy(head, 1, PLANE, plane_rows, plane, self.device(z=up)).start()
-        self.copy(head, 1, PLANE, plane_rows, plane, self.device(z=down)).start()
+        self.copy(head, 1, PLANE, split, plane, self.device(z=up)).start()
+        self.copy(head, 1, PLANE, split, plane, self.device(z=down)).start()
         self.hand_over(head, plane)
 
-    @by_width
-    def third(self, head, plane_rows):
+    @by_split
+    def third(self, head, split):
+        plane_rows = SPLITS[split][1][0]
+        every = slice(None)
+        self.arrived(head, 1, NEAR, 4, self.shard_rows - plane_rows)
+
+        def near(order, first, rows):
+            if order == "xy":
+                part = self.blocks(head, every, 1 - self.x, self.y, first, rows)
+            else:
+                part = self.blocks(head, every, self.x, 1 - self.y, first, rows)
+            to = self.across(order)[1]
+            self.copy(head, 2, NEAR, split, part, to).start()
+            self.hand_over(head, part)
+
+        self.routes(split, near)
+
+    @by_split
+    def third_plane(self, head, split):
+        plane_rows = SPLITS[split][1][0]
         every = slice(None)
         last = self.sizes[0] - 1
-        self.arrived(head, 1, NEAR, 4, self.shard_rows - plane_rows)
-
-        def near(order, first, rows):
-            if order == "xy":
-                part = self.blocks(head, every, every, self.y, first, rows)
-                to = self.device(y=1 - self.y)
-            else:
-                part = self.blocks(head, every, self.x, every, first, rows)
-                to = self.device(x=1 - self.x)
-            self.copy(head, 2, NEAR, plane_rows, part, to).start()
-            self.hand_over(head, part)
-
-        self.routes(plane_rows, near)
 
         @pl.when(self.is_end)
         def _():
@@ -447,10 +556,11 @@
             half = (last + 1) // 2
             start = jnp.where(self.z >= half, 0, half)
             part = self.blocks(head, pl.ds(start, half), every, every, 0, plane_rows)
-            self.copy(head, 2, PLANE, plane_rows, part, self.device(z=jnp.where(self.z >= half, last, 0))).start()
-
-    @by_width
-    def fourth(self, head, plane_rows):
+            self.copy(head, 2, PLANE, split, part, self.device(z=jnp.where(self.z >= half, last, 0))).start()
+
+    @by_split
+    def fourth(self, head, split):
+        plane_rows = SPLITS[split][1][0]
         every = slice(None)
         z_size = self.sizes[0]
 
@@ -469,7 +579,7 @@
                 part = self.blocks(head, every, 1 - self.x, every, first, rows)
             self.hand_over(head, part)
 
-        self.routes(plane_rows, near)
+        self.routes(split, near)
 
         for d in range(1, z_size):
             self.hand_over(head, self.blocks(head, lax.rem(self.z + d, z_size), every, every, 0, plane_rows))
@@ -491,17 +601,17 @@
 
     @scoped
     def settled(self):
-        for plane_rows in (PLANE_ROWS, WIDE_PLANE_ROWS):
+        for split, (_, (plane_rows, _)) in enumerate(SPLITS):
             near_rows = self.shard_rows - plane_rows
-            self.left(0, NEAR, plane_rows, 3, near_rows)
-            self.left(0, PLANE, plane_rows, 3, plane_rows)
-            self.left(1, NEAR, plane_rows, 4, near_rows)
-            self.left(1, PLANE, plane_rows, 8, plane_rows)
-            self.left(2, NEAR, plane_rows, 8, near_rows)
+            self.left(0, NEAR, split, 3, near_rows)
+            self.left(0, PLANE, split, 3, plane_rows)
+            self.left(1, NEAR, split, 4, near_rows)
+            self.left(1, PLANE, split, 8, plane_rows)
+            self.left(2, NEAR, split, 8, near_rows)
 
             @pl.when(jnp.logical_not(self.is_end))
             def _():
-                self.left(2, PLANE, plane_rows, 8, plane_rows)
+                self.left(2, PLANE, split, 8, plane_rows)
 
         self.handed(slice(None), self.core).wait_send()
 
@@ -537,6 +647,7 @@
     ga_v,
     gi_v,
     summary_v,
+    picked_v,
     turn_v,
     norm_gain_ref,
     attn_gain_ref,
@@ -561,7 +672,7 @@
 
     shard = [
         pltpu.make_async_copy(
-            w_hbm.at[:, pl.ds(h * HD, HD)], w_buf.at[h, ex.z, ex.x, ex.core, y], load_sem.at[12]
+            w_hbm.at[:, pl.ds(h * HD, HD)], w_buf.at[h, ex.z, ex.x, ex.core, y], load_sem.at[10]
         )
         for h in range(heads)
     ]
@@ -582,7 +693,7 @@
             )
         )
     ]
-    for copy in shard + [loads[1], loads[2], loads[6], loads[9], loads[0], *loads[3:6], loads[7], loads[8]]:
+    for copy in shard:
         copy.start()
 
     barrier = pltpu.get_barrier_semaphore()
@@ -591,13 +702,13 @@
         pl.semaphore_signal(barrier, inc=1, device_id=peer, device_id_type=MESH_ID)
 
     own_shard = w_buf.at[:, ex.z, ex.x, ex.core, y]
-    pltpu.make_async_copy(own_shard, own_shard, load_sem.at[12]).wait()
+    pltpu.make_async_copy(own_shard, own_shard, load_sem.at[10]).wait()
+    for copy in [loads[1], loads[2], loads[6], loads[9], loads[0], *loads[3:6], loads[7], loads[8]]:
+        copy.start()
     pl.semaphore_wait(barrier, len(peers))
-    ex.first_near(0)
-    for h in range(heads):
-        ex.first_plane(h)
-    ex.first_near(1)
-    ex.first_near(2)
+    lead = START.index(("kv", 0))
+    for name, head in START[:lead]:
+        getattr(ex, name)(head)
 
     quarter = HD // 4
     lane = lax.broadcasted_iota(jnp.int32, (1, 2 * quarter), 1)
@@ -629,12 +740,10 @@
         other = pltpu.roll(turned, quarter, axis=1)
         turned = turned * cosine + other * sine
 
-        def put(half, columns, values):
-            kv_v[half, rows, columns] = jnp.where(window, values, 0.0).astype(jnp.bfloat16)
-
-        put(0, slice(0, 2 * quarter), turned)
-        put(0, slice(2 * quarter, HD), full[:, 2 * quarter : HD])
-        put(1, slice(0, HD), full[:, HD:])
+        keys = jnp.concatenate([turned, full[:, 2 * quarter : HD]], axis=1)
+        first, second = (jnp.where(window, v, 0.0).astype(jnp.bfloat16) for v in (keys, full[:, HD:]))
+        cache_ref[pl.ds(place, half_len)] = jnp.where(y == 0, first, second)
+        kv_v[rows] = jnp.where(y == 0, second, first)
 
     halo_copy = pltpu.make_async_remote_copy(
         src_ref=tokens_v.at[pl.ds(local_len - HALO, HALO)],
@@ -646,7 +755,7 @@
     )
     kv_copies = [
         pltpu.make_async_remote_copy(
-            src_ref=kv_v.at[1 - y, pl.ds(k * half_len, half_len)],
+            src_ref=kv_v.at[pl.ds(k * half_len, half_len)],
             dst_ref=cache_ref.at[pl.ds(start + k * half_len, half_len)],
             send_sem=side_send.at[1 + k],
             recv_sem=side_recv.at[1 + k],
@@ -655,28 +764,23 @@
         )
         for k in range(2)
     ]
-    kept = pltpu.make_async_copy(kv_v.at[y], cache_ref.at[pl.ds(start, local_len)], load_sem.at[10])
-    loads[1].wait()
-    loads[2].wait()
-    with jax.named_scope("kv"):
-        kv_half(0)
-    loads[0].wait()
-    loads[5].wait()
-
-    @pl.when(y == 0)
-    def _():
-        halo_copy.start()
-        halo_v[...] = jnp.zeros_like(halo_v)
-
-    ex.second(0)
-    kv_copies[0].start()
-    with jax.named_scope("kv"):
-        kv_half(1)
-    ex.second(1)
-    ex.third(0)
-    ex.first_near(3)
-    kv_copies[1].start()
-    kept.start()
+
+    def take_kv(k):
+        if k == 0:
+            loads[1].wait()
+            loads[2].wait()
+        kv_half(k)
+
+    def send_kv(k):
+        kv_copies[k].start()
+
+    def send_halo(_):
+        loads[0].wait()
+
+        @pl.when(y == 0)
+        def _():
+            halo_copy.start()
+            halo_v[...] = jnp.zeros_like(halo_v)
 
     norm_step = 64
 
@@ -685,15 +789,9 @@
         rows_v[rows] = rms_norm(tokens_v[rows], norm_gain_ref[...])
         return carry
 
-    with jax.named_scope("norm"):
+    def norm(_):
+        loads[5].wait()
         lax.fori_loop(0, local_len // norm_step, norm_rows, 0)
-    ex.second(2)
-    ex.third(1)
-    ex.first_near(4)
-
-    @pl.when(y != 0)
-    def _():
-        halo_copy.wait_recv()
 
     steps = local_len // LANES_OF_TIME
     rows_ext = normed_v.shape[0]
@@ -709,17 +807,32 @@
         ).astype(jnp.bfloat16)
         return carry
 
-    lax.fori_loop(0, heads, reorder, 0)
-    edge = 2 * HALO
-    row = lax.broadcasted_iota(jnp.int32, (edge, HALO), 0)
-    col = lax.broadcasted_iota(jnp.int32, (edge, HALO), 1)
-    at = lax.div(row, LANES_OF_TIME) - (TAPS - 1)
-    early = ((lax.rem(row, LANES_OF_TIME) == 0) & (at < 0) & (at + HALO == col)).astype(jnp.bfloat16)
-    halo_rows = rms_norm(halo_v[...], norm_gain_ref[...])
-    before = jnp.dot(early, halo_rows, preferred_element_type=jnp.float32)
-    normed_v[0:edge] = (normed_v[0:edge].astype(jnp.float32) + before).astype(jnp.bfloat16)
-    ex.second(3)
-    ex.fourth(0)
+    def reorder_half(k):
+        half_heads = heads // 2
+        lax.fori_loop(*((0, half_heads) if k == 0 else (half_heads, heads)), reorder, 0)
+        if k == 0:
+            return
+
+        @pl.when(y != 0)
+        def _():
+            halo_copy.wait_recv()
+
+        edge = 2 * HALO
+        row = lax.broadcasted_iota(jnp.int32, (edge, HALO), 0)
+        col = lax.broadcasted_iota(jnp.int32, (edge, HALO), 1)
+        at = lax.div(row, LANES_OF_TIME) - (TAPS - 1)
+        early = (lax.rem(row, LANES_OF_TIME) == 0) & (at < 0) & (at + HALO == col)
+        halo_rows = rms_norm(halo_v[...], norm_gain_ref[...])
+        before = jnp.dot(early.astype(jnp.bfloat16), halo_rows, preferred_element_type=jnp.float32)
+        normed_v[0:edge] = (normed_v[0:edge].astype(jnp.float32) + before).astype(jnp.bfloat16)
+
+    tasks = {"kv": take_kv, "send_kv": send_kv, "halo": send_halo, "norm": norm, "reorder": reorder_half}
+    for name, head in START[lead:]:
+        if name in tasks:
+            with jax.named_scope(name):
+                tasks[name](head)
+        else:
+            getattr(ex, name)(head)
     for copy in (loads[3], loads[4], loads[7], loads[8]):
         copy.wait()
 
@@ -738,15 +851,7 @@
     inner = lax.broadcasted_iota(jnp.int32, (STEP_ROWS, HD), 0)
     first_at = start + lax.rem(inner, LANES_OF_TIME) * steps + lax.div(inner, LANES_OF_TIME)
 
-    def head_step(head, carry):
-        ex.ready(head)
-
-        for lag, stage in ((5, ex.first_near), (4, ex.second), (2, ex.third)):
-
-            @pl.when(head + lag < heads)
-            def _():
-                stage(head + lag)
-
+    def project(head):
         columns = pl.ds(pl.multiple_of(head * HD, HD), HD)
         w_block = w_buf[head].reshape(normed_v.shape[1], HD)
         projected = jnp.dot(
@@ -769,11 +874,10 @@
         xc_v[...] = x_conv.astype(jnp.float32)
         ga_v[...] = jnp.dot(x_conv, wa_v[head], preferred_element_type=jnp.float32)
         gi_v[...] = jnp.dot(x_conv, wi_v[head], preferred_element_type=jnp.float32)
-
-        @pl.when(head + 1 < heads)
-        def _():
-            ex.fourth(head + 1)
-
+        picked_v[...] = picked[0:LANES_OF_TIME]
+
+    def scan(head):
+        columns = pl.ds(pl.multiple_of(head * HD, HD), HD)
         rate = -8.0 * jax.nn.softplus(-decay_ref[:, columns])
 
         def block(i, carry):
@@ -805,21 +909,33 @@
         keep_total = jnp.exp(jnp.sum(rate_sum, axis=0, keepdims=True))
         place = lax.broadcasted_iota(jnp.int32, (LANES_OF_TIME, HD), 0)
         summary_v[head] = jnp.where(
-            place == 0, keep_total, jnp.where(place == 1, total, picked[0:LANES_OF_TIME])
+            place == 0, keep_total, jnp.where(place == 1, total, picked_v[...])
         )
 
         @pl.when(lax.div(head, per_owner) != y)
         def _():
             summary_copy(head, lax.rem(head, per_owner)).start()
 
+    def take(steps):
+        for name, head in steps:
+            if name in tasks:
+                with jax.named_scope(name):
+                    tasks[name](head)
+            else:
+                getattr(ex, name)(head)
+
+    def head_step(head, carry):
+        for slot, (name, task) in enumerate((("project", project), ("scan", scan))):
+            for at, steps in enumerate(SLOTS):
+                if steps[slot]:
+                    pl.when(head == at)(functools.partial(take, steps[slot]))
+            with jax.named_scope(name):
+                task(head)
         return carry
 
     lax.fori_loop(0, heads, head_step, 0)
 
-    own = pltpu.make_async_copy(
-        summary_v.at[pl.ds(y * per_owner, per_owner)], own_ref, load_sem.at[11]
-    )
-    own.start()
+    own_ref[...] = summary_v[pl.ds(y * per_owner, per_owner)]
     every = summary_v.at[pl.ds(0, per_owner)]
     exchanged = pltpu.make_async_remote_copy(
         src_ref=every,
@@ -831,7 +947,6 @@
     )
     for copy in kv_copies:
         copy.wait()
-    kept.wait()
 
     @pl.when(y == 0)
     def _():
@@ -839,45 +954,23 @@
 
     ex.settled()
     with jax.named_scope("exchanged"):
-        own.wait()
         exchanged.wait()
 
 
 def finish_kernel(
-    own_hbm,
-    theirs_hbm,
-    kv_hbm,
-    state_hbm,
-    conv_hbm,
-    cache_hbm,
-    zeros_v,
-    kv_v,
-    own_v,
-    theirs_v,
-    state_v,
-    conv_v,
-    in_sem,
-    out_sem,
+    own_ref, theirs_ref, kv_ref, state_hbm, conv_hbm, cache_hbm, zeros_v, state_v, conv_v, out_sem
 ):
-    rest = kv_v.shape[0]
-    load_own = pltpu.make_async_copy(own_hbm, own_v, in_sem.at[0])
-    load_theirs = pltpu.make_async_copy(theirs_hbm, theirs_v, in_sem.at[1])
-    load_kv = pltpu.make_async_copy(kv_hbm, kv_v, in_sem.at[2])
-    for copy in (load_own, load_theirs, load_kv):
-        copy.start()
-    zeros_v[...] = jnp.zeros_like(zeros_v)
+    rest = kv_ref.shape[0]
     store = [
-        pltpu.make_async_copy(zeros_v, cache_hbm.at[pl.ds(rest, zeros_v.shape[0])], out_sem.at[0]),
-        pltpu.make_async_copy(kv_v, cache_hbm.at[pl.ds(0, rest)], out_sem.at[1]),
+        pltpu.make_async_copy(kv_ref, cache_hbm.at[pl.ds(0, rest)], out_sem.at[0]),
+        pltpu.make_async_copy(zeros_v, cache_hbm.at[pl.ds(rest, zeros_v.shape[0])], out_sem.at[1]),
         pltpu.make_async_copy(state_v, state_hbm, out_sem.at[2]),
         pltpu.make_async_copy(conv_v, conv_hbm, out_sem.at[3]),
     ]
     store[0].start()
-    load_own.wait()
-    load_theirs.wait()
     first_half = lax.axis_index("seq") == 0
-    for k in range(own_v.shape[0]):
-        own, got = own_v[k], theirs_v[k]
+    for k in range(own_ref.shape[0]):
+        own, got = own_ref[k], theirs_ref[k]
         head_part = jnp.where(first_half, own, got)
         tail_part = jnp.where(first_half, got, own)
         columns = slice(k * HD, (k + 1) * HD)
@@ -886,7 +979,7 @@
         conv_v[0, :, columns] = picked.astype(jnp.bfloat16)
     store[2].start()
     store[3].start()
-    load_kv.wait()
+    zeros_v[...] = jnp.zeros_like(zeros_v)
     store[1].start()
     for copy in store:
         copy.wait()
@@ -900,17 +993,18 @@
     heads = width // HD
     rows_ext = -(-(local_len + (TAPS - 1) * LANES_OF_TIME) // HALO) * HALO
     anywhere = pl.BlockSpec(memory_space=pl.ANY)
+    vmem = pl.BlockSpec(memory_space=pltpu.VMEM)
     owned = width // seq_parts
     per_owner = heads // seq_parts
     half = w_kv.shape[1] // seq_parts
     own, theirs, kv = pl.pallas_call(
         functools.partial(prefill_kernel, sizes),
-        in_specs=[anywhere] * 11,
-        out_specs=(anywhere, anywhere, anywhere),
+        in_specs=[pl.BlockSpec(memory_space=pltpu.HBM)] * 11,
+        out_specs=(vmem, vmem, vmem),
         out_shape=(
-            jax.ShapeDtypeStruct((per_owner, LANES_OF_TIME, HD), jnp.float32),
-            jax.ShapeDtypeStruct((per_owner, LANES_OF_TIME, HD), jnp.float32),
-            jax.ShapeDtypeStruct((seq_parts * local_len, half), jnp.bfloat16),
+            pltpu.VMEM((per_owner, LANES_OF_TIME, HD), jnp.float32),
+            pltpu.VMEM((per_owner, LANES_OF_TIME, HD), jnp.float32),
+            pltpu.VMEM((seq_parts * local_len, half), jnp.bfloat16),
         ),
         scratch_shapes=[
             pltpu.VMEM((heads, z_size, x_size, cores, seq_parts, w_x.shape[0], HD), jnp.bfloat16),
@@ -922,23 +1016,24 @@
             pltpu.VMEM((HALO, width), jnp.bfloat16),
             pltpu.VMEM((local_len, width), jnp.bfloat16),
             pltpu.VMEM((rows_ext, width), jnp.bfloat16),
-            pltpu.VMEM((2, local_len, half), jnp.bfloat16),
+            pltpu.VMEM((local_len, half), jnp.bfloat16),
             pltpu.VMEM((rows_ext, HD), jnp.float32),
             pltpu.VMEM((local_len, HD), jnp.float32),
             pltpu.VMEM((local_len, HD), jnp.float32),
             pltpu.VMEM((local_len, HD), jnp.float32),
             pltpu.VMEM((heads, LANES_OF_TIME, HD), jnp.float32),
+            pltpu.VMEM((LANES_OF_TIME, HD), jnp.float32),
             pltpu.VMEM((2, local_len // 2, HD // 2), jnp.float32),
             pltpu.VMEM((1, width), jnp.float32),
             pltpu.VMEM((1, width), jnp.float32),
             pltpu.VMEM((1, width), jnp.float32),
             pltpu.VMEM(conv_w.shape, jnp.float32),
             pltpu.SMEM((1,), jnp.int32),
-            pltpu.SemaphoreType.DMA((3, 2, 2)),
+            pltpu.SemaphoreType.DMA((3, 2, len(SPLITS))),
             pltpu.SemaphoreType.DMA((heads, 4)),
             pltpu.SemaphoreType.DMA((1,)),
             pltpu.SemaphoreType.DMA((heads,)),
-            pltpu.SemaphoreType.DMA((13,)),
+            pltpu.SemaphoreType.DMA((11,)),
             pltpu.SemaphoreType.DMA((4,)),
             pltpu.SemaphoreType.DMA((4,)),
         ],
@@ -961,7 +1056,7 @@
     state_shape, conv_shape = (1, owned), (1, TAPS - 1, owned)
     state, conv_state, cache = pl.pallas_call(
         finish_kernel,
-        in_specs=[anywhere] * 3,
+        in_specs=[vmem] * 3,
         out_specs=(anywhere, anywhere, anywhere),
         out_shape=(
             jax.ShapeDtypeStruct(state_shape, jnp.float32),
@@ -970,15 +1065,11 @@
         ),
         scratch_shapes=[
             pltpu.VMEM((W - kv.shape[0], half), jnp.bfloat16),
-            pltpu.VMEM(kv.shape, jnp.bfloat16),
-            pltpu.VMEM(own.shape, jnp.float32),
-            pltpu.VMEM(own.shape, jnp.float32),
             pltpu.VMEM(state_shape, jnp.float32),
             pltpu.VMEM(conv_shape, jnp.bfloat16),
-            pltpu.SemaphoreType.DMA((3,)),
             pltpu.SemaphoreType.DMA((4,)),
         ],
-    )(own, theirs, kv)
+    )(*(pltpu.with_memory_space_constraint(v, pltpu.VMEM) for v in (own, theirs, kv)))
     return state, conv_state, cache[None]
 
 
@@ -992,7 +1083,8 @@
         length < W
         and width % (HD * seq_parts) == 0
         and w_x.shape[0] % (devices * HALO) == 0
-        and w_x.shape[0] // devices > WIDE_PLANE_ROWS
+        and w_x.shape[0] // devices > max(p + q for _, (p, q) in SPLITS)
+        and width // HD == sum(n for n, _ in SPLITS) == len(SLOTS)
         and w_kv.shape[1] == seq_parts * HD
         and tokens.shape[0] == mesh.shape["batch"]
     )

time: 71.6 us -> 71 us (level)
  no operation moved by 1% of the time
where the time goes in v3:
time: 71 us; the launch traced here: 70.8 us
  Pallas kernels  69.6 us (98%)
  between operations  1.29 us (2%)
    pallas_call x1, Pallas kernels, gathered_on_device(): pl.pallas_call(functools.partial(prefill_kernel, sizes), in_specs=[pl.Blo...  68.5 us

profile of v3, /device:TPU:0, one launch (start us, length us, event | category | flops | bytes accessed | tf_op | source)
XLA Modules:
  0.0 70.8 jit_solution(4902170671877866353)
XLA Ops:
  1.3 68.5 %shard_map.130 = (f32[5,8,256]{2,1,0:T(8,128)S(1)}, f32[5,8,256]{2,1,0:T(8,128)S(1)}, bf16[1024,256]{1,0:T(8,128)(2,1)S(1)}) custom-call(s32[1]{0:T(128)S(6)} %copy.14.length_hbm, bf16[512,2560]{1,0:T(8,128)(2,1)} %bitcast.3, bf16[512,2560]{1,0:T(8,128)(2,1)} %bitcast.4, f32[2560]{0:T(1024)} %norm_gain_hbm.1, f32[2560]{0:T(1024)} %attn_gain_hbm.1, ...), custom_call_target="tpu_custom_call" | custom-call | tf_op jit(solution)/shard_map/pallas_call | solution.py:1000
  69.8 1.0 %shard_map.131 = (f32[1,1280]{1,0:T(1,128)}, bf16[1,3,1280]{2,1,0:T(4,128)(2,1)}, bf16[2048,256]{1,0:T(8,128)(2,1)}) custom-call(f32[5,8,256]{2,1,0:T(8,128)S(1)} %get-tuple-element.9.own_ref, f32[5,8,256]{2,1,0:T(8,128)S(1)} %get-tuple-element.10.theirs_ref, bf16[1024,256]{1,0:T(8,128)(2,1)S(1)} %get-tuple-element.11.kv_ref), custom_call_target="tpu_custom_call" | custom-call | tf_op jit(solution)/shard_map/pallas_call | solution.py:1057

commit v4 on v3

--- a/solution.py
+++ b/solution.py
@@ -241,49 +241,53 @@
 
 
 MESH_ID = pl.DeviceIdType.MESH
-SPLITS = ((6, (16, 16)), (4, (16, 0)),)
+SPLITS = ((10, (16, 16)),)
 NEAR, PLANE = 0, 1
+EDGE = 8
 START = (
-    ("plane", 0), ("near", 1), ("own", 0), ("own", 4), ("own", 1), ("plane", 1), ("near", 0), ("plane", 2),
-    ("own", 3), ("kv", 0), ("halo", 0), ("send_kv", 0), ("own", 2), ("plane", 3), ("near", 2), ("kv", 1),
-    ("second", 0), ("near", 3), ("norm", 0), ("second", 1), ("plane", 4), ("third_plane", 0), ("second", 2),
-    ("reorder", 0), ("near", 4), ("third", 0), ("second", 3), ("send_kv", 1), ("third", 1), ("third_plane", 1),
-    ("plane", 6), ("reorder", 1),
+    ("near", 0), ("plane", 0), ("own", 0), ("near", 1), ("plane", 1), ("own", 1), ("near", 2), ("plane", 2),
+    ("own", 2), ("plane", 3), ("own", 3), ("plane", 4), ("own", 4), ("kv", 0), ("halo", 0), ("second", 0),
+    ("near", 3), ("send_kv", 0), ("kv", 1), ("second", 1), ("third", 0), ("send_kv", 1), ("norm", 0), ("near", 4),
+    ("second", 2), ("third_plane", 0), ("third", 1), ("reorder", 0), ("second", 3), ("third_plane", 1),
+    ("reorder", 1),
 )
 SLOTS = (
     (
         (
-            ("plane", 5), ("plane", 7), ("fourth", 0), ("third", 2), ("third", 3), ("third_plane", 2), ("near", 5),
-            ("own", 7), ("own", 5), ("second", 4), ("fourth", 1), ("ready", 0),
-        ),
-        (),
+            ("fourth", 0), ("ready", 0), ("near", 5), ("plane", 5), ("own", 5), ("second", 4), ("third_plane", 2),
+            ("third", 2),
+        ),
+        (
+            ("fourth", 1),
+        ),
     ),
     (
         (
-            ("own", 6), ("plane", 8), ("third_plane", 3), ("near", 6), ("second", 5), ("fourth", 2), ("ready", 1),
-        ),
-        (
-            ("plane", 9), ("third", 4),
+            ("ready", 1), ("near", 6), ("plane", 6), ("own", 6), ("second", 5), ("third_plane", 3), ("third", 3),
+        ),
+        (
+            ("fourth", 2),
         ),
     ),
     (
         (
-            ("near", 7), ("third_plane", 4), ("second", 6), ("third", 5), ("ready", 2), ("fourth", 3),
-        ),
-        (),
+            ("ready", 2), ("near", 7), ("plane", 7), ("own", 7), ("second", 6), ("third_plane", 4), ("third", 4),
+        ),
+        (
+            ("fourth", 3),
+        ),
     ),
     (
         (
-            ("own", 8), ("near", 8), ("third_plane", 5), ("third_plane", 6), ("second", 7), ("ready", 3),
-            ("third", 6),
-        ),
-        (
-            ("fourth", 4), ("own", 9),
+            ("ready", 3), ("near", 8), ("plane", 8), ("own", 8), ("second", 7), ("third_plane", 5), ("third", 5),
+        ),
+        (
+            ("fourth", 4),
         ),
     ),
     (
         (
-            ("near", 9), ("third", 7), ("second", 8), ("ready", 4),
+            ("ready", 4), ("near", 9), ("plane", 9), ("own", 9), ("second", 8), ("third_plane", 6), ("third", 6),
         ),
         (
             ("fourth", 5),
@@ -291,23 +295,23 @@
     ),
     (
         (
-            ("third_plane", 7), ("fourth", 6), ("ready", 5), ("second", 9),
-        ),
-        (
-            ("third", 8),
+            ("ready", 5), ("second", 9), ("third_plane", 7), ("third", 7),
+        ),
+        (
+            ("fourth", 6),
         ),
     ),
     (
         (
-            ("fourth", 7), ("ready", 6), ("third_plane", 8),
-        ),
-        (
-            ("third", 9),
+            ("ready", 6), ("third_plane", 8), ("third", 8),
+        ),
+        (
+            ("fourth", 7),
         ),
     ),
     (
         (
-            ("third_plane", 9), ("ready", 7),
+            ("ready", 7), ("third_plane", 9), ("third", 9),
         ),
         (
             ("fourth", 8),
@@ -315,9 +319,11 @@
     ),
     (
         (
-            ("ready", 8), ("fourth", 9),
-        ),
-        (),
+            ("ready", 8),
+        ),
+        (
+            ("fourth", 9),
+        ),
     ),
     (
         (
@@ -746,7 +752,7 @@
         kv_v[rows] = jnp.where(y == 0, second, first)
 
     halo_copy = pltpu.make_async_remote_copy(
-        src_ref=tokens_v.at[pl.ds(local_len - HALO, HALO)],
+        src_ref=tokens_v.at[pl.ds(local_len - EDGE, EDGE)],
         dst_ref=halo_v,
         send_sem=side_send.at[0],
         recv_sem=side_recv.at[0],
@@ -818,10 +824,10 @@
             halo_copy.wait_recv()
 
         edge = 2 * HALO
-        row = lax.broadcasted_iota(jnp.int32, (edge, HALO), 0)
-        col = lax.broadcasted_iota(jnp.int32, (edge, HALO), 1)
+        row = lax.broadcasted_iota(jnp.int32, (edge, EDGE), 0)
+        col = lax.broadcasted_iota(jnp.int32, (edge, EDGE), 1)
         at = lax.div(row, LANES_OF_TIME) - (TAPS - 1)
-        early = (lax.rem(row, LANES_OF_TIME) == 0) & (at < 0) & (at + HALO == col)
+        early = (lax.rem(row, LANES_OF_TIME) == 0) & (at < 0) & (at + EDGE == col)
         halo_rows = rms_norm(halo_v[...], norm_gain_ref[...])
         before = jnp.dot(early.astype(jnp.bfloat16), halo_rows, preferred_element_type=jnp.float32)
         normed_v[0:edge] = (normed_v[0:edge].astype(jnp.float32) + before).astype(jnp.bfloat16)
@@ -854,8 +860,13 @@
     def project(head):
         columns = pl.ds(pl.multiple_of(head * HD, HD), HD)
         w_block = w_buf[head].reshape(normed_v.shape[1], HD)
-        projected = jnp.dot(
-            normed_v[...], w_block, preferred_element_type=jnp.float32
+        half_rows = rows_ext // 4
+        projected = jnp.concatenate(
+            [
+                jnp.dot(normed_v[k * half_rows : (k + 1) * half_rows], w_block, preferred_element_type=jnp.float32)
+                for k in range(4)
+            ],
+            axis=0,
         ).astype(jnp.bfloat16)
         xp_v[...] = projected.astype(jnp.float32)
         row = lax.broadcasted_iota(jnp.int32, (HALO, rows_ext), 1)
@@ -1013,7 +1024,7 @@
             pltpu.VMEM(w_kv.shape, jnp.bfloat16),
             pltpu.VMEM(w_a.shape, jnp.bfloat16),
             pltpu.VMEM(w_i.shape, jnp.bfloat16),
-            pltpu.VMEM((HALO, width), jnp.bfloat16),
+            pltpu.VMEM((EDGE, width), jnp.bfloat16),
             pltpu.VMEM((local_len, width), jnp.bfloat16),
             pltpu.VMEM((rows_ext, width), jnp.bfloat16),
             pltpu.VMEM((local_len, half), jnp.bfloat16),

time: 71 us -> 69.6 us (0.980)
  Pallas kernels: 69.6 us -> 68.1 us
    pallas_call x1, Pallas kernels: 68.5 us -> 67.1 us  [gathered_on_device(): pl.pallas_call(functools.partial(prefill_kernel, sizes), in_specs=[pl.Blo...]
where the time goes in v4:
time: 69.6 us; the launch traced here: 69.4 us
  Pallas kernels  68.1 us (98%)
  between operations  1.29 us (2%)
    pallas_call x1, Pallas kernels, gathered_on_device(): pl.pallas_call(functools.partial(prefill_kernel, sizes), in_specs=[pl.Blo...  67.1 us

profile of v4, /device:TPU:0, one launch (start us, length us, event | category | flops | bytes accessed | tf_op | source)
XLA Modules:
  0.0 69.4 jit_solution(11497315659597038950)
XLA Ops:
  1.3 67.1 %shard_map.130 = (f32[5,8,256]{2,1,0:T(8,128)S(1)}, f32[5,8,256]{2,1,0:T(8,128)S(1)}, bf16[1024,256]{1,0:T(8,128)(2,1)S(1)}) custom-call(s32[1]{0:T(128)S(6)} %copy.14.length_hbm, bf16[512,2560]{1,0:T(8,128)(2,1)} %bitcast.3, bf16[512,2560]{1,0:T(8,128)(2,1)} %bitcast.4, f32[2560]{0:T(1024)} %norm_gain_hbm.1, f32[2560]{0:T(1024)} %attn_gain_hbm.1, ...), custom_call_target="tpu_custom_call" | custom-call | tf_op jit(solution)/shard_map/pallas_call | solution.py:1011
  68.4 1.0 %shard_map.131 = (f32[1,1280]{1,0:T(1,128)}, bf16[1,3,1280]{2,1,0:T(4,128)(2,1)}, bf16[2048,256]{1,0:T(8,128)(2,1)}) custom-call(f32[5,8,256]{2,1,0:T(8,128)S(1)} %get-tuple-element.9.own_ref, f32[5,8,256]{2,1,0:T(8,128)S(1)} %get-tuple-element.10.theirs_ref, bf16[1024,256]{1,0:T(8,128)(2,1)S(1)} %get-tuple-element.11.kv_ref), custom_call_target="tpu_custom_call" | custom-call | tf_op jit(solution)/shard_map/pallas_call | solution.py:1068

commit v5 on v4

--- a/solution.py
+++ b/solution.py
@@ -254,51 +254,50 @@
 SLOTS = (
     (
         (
-            ("fourth", 0), ("ready", 0), ("near", 5), ("plane", 5), ("own", 5), ("second", 4), ("third_plane", 2),
-            ("third", 2),
-        ),
-        (
-            ("fourth", 1),
+            ("fourth", 0), ("ready", 0), ("near", 5), ("third_plane", 2), ("third", 2),
+        ),
+        (
+            ("fourth", 1), ("plane", 5), ("own", 5), ("second", 4),
         ),
     ),
     (
         (
-            ("ready", 1), ("near", 6), ("plane", 6), ("own", 6), ("second", 5), ("third_plane", 3), ("third", 3),
-        ),
-        (
-            ("fourth", 2),
+            ("ready", 1), ("near", 6), ("third_plane", 3), ("third", 3),
+        ),
+        (
+            ("fourth", 2), ("plane", 6), ("own", 6), ("second", 5),
         ),
     ),
     (
         (
-            ("ready", 2), ("near", 7), ("plane", 7), ("own", 7), ("second", 6), ("third_plane", 4), ("third", 4),
-        ),
-        (
-            ("fourth", 3),
+            ("ready", 2), ("near", 7), ("third_plane", 4), ("third", 4),
+        ),
+        (
+            ("fourth", 3), ("plane", 7), ("own", 7), ("second", 6),
         ),
     ),
     (
         (
-            ("ready", 3), ("near", 8), ("plane", 8), ("own", 8), ("second", 7), ("third_plane", 5), ("third", 5),
-        ),
-        (
-            ("fourth", 4),
+            ("ready", 3), ("near", 8), ("third_plane", 5), ("third", 5),
+        ),
+        (
+            ("fourth", 4), ("plane", 8), ("own", 8), ("second", 7),
         ),
     ),
     (
         (
-            ("ready", 4), ("near", 9), ("plane", 9), ("own", 9), ("second", 8), ("third_plane", 6), ("third", 6),
-        ),
-        (
-            ("fourth", 5),
+            ("ready", 4), ("near", 9), ("third_plane", 6), ("third", 6),
+        ),
+        (
+            ("fourth", 5), ("plane", 9), ("own", 9), ("second", 8),
         ),
     ),
     (
         (
-            ("ready", 5), ("second", 9), ("third_plane", 7), ("third", 7),
-        ),
-        (
-            ("fourth", 6),
+            ("ready", 5), ("third_plane", 7), ("third", 7),
+        ),
+        (
+            ("fourth", 6), ("second", 9),
         ),
     ),
     (

time: 69.6 us -> 68.6 us (0.986)
  Pallas kernels: 68.1 us -> 67.1 us
    pallas_call x1, Pallas kernels: 67.1 us -> 66.1 us  [gathered_on_device(): pl.pallas_call(functools.partial(prefill_kernel, sizes), in_specs=[pl.Blo...]
where the time goes in v5:
time: 68.6 us; the launch traced here: 68.4 us
  Pallas kernels  67.1 us (98%)
  between operations  1.29 us (2%)
    pallas_call x1, Pallas kernels, gathered_on_device(): pl.pallas_call(functools.partial(prefill_kernel, sizes), in_specs=[pl.Blo...  66.1 us

profile of v5, /device:TPU:0, one launch (start us, length us, event | category | flops | bytes accessed | tf_op | source)
XLA Modules:
  0.0 68.4 jit_solution(7591518711748272650)
XLA Ops:
  1.3 66.1 %shard_map.130 = (f32[5,8,256]{2,1,0:T(8,128)S(1)}, f32[5,8,256]{2,1,0:T(8,128)S(1)}, bf16[1024,256]{1,0:T(8,128)(2,1)S(1)}) custom-call(s32[1]{0:T(128)S(6)} %copy.14.length_hbm, bf16[512,2560]{1,0:T(8,128)(2,1)} %bitcast.3, bf16[512,2560]{1,0:T(8,128)(2,1)} %bitcast.4, f32[2560]{0:T(1024)} %norm_gain_hbm.1, f32[2560]{0:T(1024)} %attn_gain_hbm.1, ...), custom_call_target="tpu_custom_call" | custom-call | tf_op jit(solution)/shard_map/pallas_call | solution.py:1010
  67.4 1.0 %shard_map.131 = (f32[1,1280]{1,0:T(1,128)}, bf16[1,3,1280]{2,1,0:T(4,128)(2,1)}, bf16[2048,256]{1,0:T(8,128)(2,1)}) custom-call(f32[5,8,256]{2,1,0:T(8,128)S(1)} %get-tuple-element.9.own_ref, f32[5,8,256]{2,1,0:T(8,128)S(1)} %get-tuple-element.10.theirs_ref, bf16[1024,256]{1,0:T(8,128)(2,1)S(1)} %get-tuple-element.11.kv_ref), custom_call_target="tpu_custom_call" | custom-call | tf_op jit(solution)/shard_map/pallas_call | solution.py:1067
